TPU v7x, 32 devices: a whole 2x2x4 slice. The times are simulated.
32 devices in a mesh: fsdp: 4 (over y, core), sp: 8 (over z, x).
Axes of the slice: x: 2, y: 2, z: 4, core: 2. Of those that a mesh axis runs over, the one named last changes fastest.
Arguments:
- hidden: bfloat16 [2048, 8192], P('sp', 'fsdp'), may hold values from -23 to 23
- w_query: bfloat16 [8192, 1024], P('fsdp', 'sp'), may hold values from -0.125 to 0.125
- w_keyvalue: bfloat16 [8192, 256], P('fsdp', 'sp'), may hold values from -0.125 to 0.125
- w_output: bfloat16 [1024, 8192], P('sp', 'fsdp'), may hold values from -0.75 to 0.75
- segment_ids: int32 [2048], P('sp'), may hold values from 0 to 7, never falling along the last dimension, each value on 1 to 512 neighbouring positions
Outputs:
- attended: bfloat16 [2048, 8192], P('sp', 'fsdp')
Inputs may be any that keep to these rules, and one draw needn't show every extreme that they name: `segment_ids`: segment ids never fall along the sequence; every episode has between 1 and 512 tokens.
All inputs are finite; a program needn't handle non-finite values.
Results may differ from a plain program's by a relative error of at most 0.0085.
The roundings to bfloat16 on the way count: a program that leaves them out, or rounds other values in their place, can miss the bound.
Values may be sent and summed in bfloat16 or wider, within the bound.
A program may use at most 128 MiB of HBM per device.

v0:
```python
import functools
import math

import jax
import jax.numpy as jnp
from jax import lax
from jax.experimental import pallas as pl
from jax.experimental.pallas import tpu as pltpu
from jax.sharding import PartitionSpec as P

HD = 128
GROUP = 8


ROPE_BASE = 500000.0
NEG_FILL = -1e30


def rotate(values, positions, head_count, width):
    row_count = values.shape[0]
    shaped = values.reshape(row_count, head_count, width)
    half_width = width // 2
    frequency = jnp.exp(
        jnp.arange(half_width, dtype=jnp.float32) * (-2.0 * math.log(ROPE_BASE) / width)
    )
    angles = positions.astype(jnp.float32)[:, None] * frequency[None, :]
    cosine = jnp.cos(angles)[:, None, :]
    sine_part = jnp.sin(angles)[:, None, :]
    lower_half = shaped[:, :, :half_width]
    upper_half = shaped[:, :, half_width:]
    turned = jnp.concatenate(
        [
            lower_half * cosine - upper_half * sine_part,
            upper_half * cosine + lower_half * sine_part,
        ],
        axis=2,
    )
    return turned.reshape(row_count, head_count * width)


def split_keys(kv_sum, positions, kv_count, width):
    row_count = kv_sum.shape[0]
    shaped = kv_sum.reshape(row_count, kv_count, 2, width)
    key_part = rotate(
        shaped[:, :, 0, :].reshape(row_count, kv_count * width), positions, kv_count, width
    )
    key_part = key_part.reshape(row_count, kv_count, 1, width)
    return jnp.concatenate([key_part, shaped[:, :, 1:2, :]], axis=2).astype(jnp.bfloat16)


def merge_keys(
    state_in, query_tile, query_pos_tile, query_seg_tile, key_tile, key_pos_tile, key_seg_tile
):
    running_max, running_sum, weighted = state_in
    allowed = (key_pos_tile[None, :] <= query_pos_tile[:, None]) & (
        key_seg_tile[None, :] == query_seg_tile[:, None]
    )
    key_part = key_tile[:, :HD]
    value_part = key_tile[:, HD:]
    scores = lax.dot_general(
        query_tile, key_part, (((1,), (1,)), ((), ())), preferred_element_type=jnp.float32
    ) * HD ** (-0.5)
    masked = jnp.where(allowed, scores, NEG_FILL)
    new_max = jnp.maximum(running_max, jnp.max(masked, axis=1))
    weights = jnp.where(allowed, jnp.exp(masked - new_max[:, None]), 0.0)
    new_sum = jnp.sum(weights, axis=1)
    new_weighted = jnp.dot(
        weights.astype(jnp.bfloat16), value_part, preferred_element_type=jnp.float32
    )
    return (new_max, new_sum, new_weighted)


def on_device(hidden, w_query, w_keyvalue, w_output, segment_ids):
    fsdp_count = lax.axis_size("fsdp")
    seq_count = lax.axis_size("sp")
    fsdp_index = lax.axis_index("fsdp")
    seq_index = lax.axis_index("sp")
    tok_rows = hidden.shape[0]
    sub_rows = tok_rows // fsdp_count
    kv_count = seq_count // GROUP
    query_rows = seq_count * sub_rows
    offsets = jnp.arange(query_rows, dtype=jnp.int32)
    query_pos = offsets // sub_rows * tok_rows + fsdp_index * sub_rows + offsets % sub_rows
    own_positions = (
        seq_index * tok_rows + fsdp_index * sub_rows + jnp.arange(sub_rows, dtype=jnp.int32)
    )

    def project(weight_block):
        return jnp.dot(hidden, weight_block, preferred_element_type=jnp.float32)

    query_part = project(lax.all_gather(w_query, "sp", axis=1, tiled=True))
    kv_part = project(lax.all_gather(w_keyvalue, "sp", axis=1, tiled=True))
    query_sum, kv_sum = (
        lax.psum_scatter(query_part, "fsdp", scatter_dimension=0, tiled=True),
        lax.psum_scatter(kv_part, "fsdp", scatter_dimension=0, tiled=True),
    )
    query_local = rotate(query_sum, own_positions, seq_count, HD).astype(jnp.bfloat16)
    pairs = split_keys(kv_sum, own_positions, kv_count, HD)
    expanded = jnp.repeat(pairs, GROUP, axis=1).reshape(sub_rows, seq_count * 2 * HD)
    query_head, kv_head = (
        lax.all_to_all(query_local, "sp", split_axis=1, concat_axis=0, tiled=True),
        lax.all_to_all(expanded, "sp", split_axis=1, concat_axis=0, tiled=True),
    )
    segment_all = lax.all_gather(segment_ids, "sp", axis=0, tiled=True)
    query_seg = segment_all[query_pos]
    initial = (
        jnp.full((query_rows,), NEG_FILL, jnp.float32),
        jnp.zeros((query_rows,), jnp.float32),
        jnp.zeros((query_rows, HD), jnp.float32),
    )
    block_keys = lax.all_gather(kv_head, "fsdp", axis=0, tiled=True)
    piece_rows = block_keys.shape[0]
    row_ids = jnp.arange(piece_rows, dtype=jnp.int32)
    source_id = row_ids // query_rows
    within = row_ids % query_rows
    key_pos = within // sub_rows * tok_rows + source_id * sub_rows + within % sub_rows
    key_seg = segment_all[key_pos]
    final_max, final_sum, final_weighted = merge_keys(
        initial, query_head, query_pos, query_seg, block_keys, key_pos, key_seg
    )
    attention = (final_weighted / final_sum[:, None]).astype(jnp.bfloat16)
    back_rows = lax.all_to_all(attention, "sp", split_axis=0, concat_axis=1, tiled=True)
    mixed_rows = lax.all_gather(back_rows, "fsdp", axis=0, tiled=True)
    result = jnp.dot(
        mixed_rows,
        lax.all_gather(w_output, "sp", axis=0, tiled=True),
        preferred_element_type=jnp.float32,
    )
    return result.astype(jnp.bfloat16)


NEG_POS = -1
WO_CHUNKS = 4


def fused_kernel(
    nf, nz, nx, hid, wq, wkv, wo, seg, out,
    h_buf, wq_buf, wkv_buf, wo_buf, seg_buf,
    q_part, q_recv, kv_part, kv_recv, kv_piece, kv_all, mix_own, mix_buf, q_cos, q_sin,
    s_loc, s_hid, r_hid, s_seg, r_seg, s_wkv, r_wkv, s_wqr, s_wql, r_wq,
    s_q, r_q, s_kvp, r_kvp, s_kv, r_kv, s_wor, s_wol, s_wox, r_wo, s_mix, r_mix,
):
    f = lax.axis_index("fsdp")
    s = lax.axis_index("sp")
    z, x = s // nx, s % nx
    tok, kdim = hid.shape
    rows = tok * nx
    sub = rows // nf
    kvw = wkv.shape[0]
    other = 1 - x
    chunk = wo.shape[1] // WO_CHUNKS
    f32, bf16 = jnp.float32, jnp.bfloat16

    def dev(ff, zz, xx):
        return (ff, zz * nx + xx)

    def remote(src, dst, ss, rs, target):
        return pltpu.make_async_remote_copy(
            src_ref=src, dst_ref=dst, send_sem=ss, recv_sem=rs,
            device_id=target, device_id_type=pl.DeviceIdType.MESH,
        )

    def tile(ref, count):
        return pl.ds(pl.multiple_of(ref * count, count), count)

    here = (f, s)
    own_h = pltpu.make_async_copy(hid, h_buf.at[tile(x, tok)], s_loc.at[0])
    own_wq = pltpu.make_async_copy(wq, wq_buf.at[z], s_loc.at[1])
    own_wkv = pltpu.make_async_copy(wkv, wkv_buf.at[tile(z, kvw)], s_loc.at[2])
    own_wo = pltpu.make_async_copy(wo, wo_buf.at[tile(s, HD)], s_loc.at[3])
    own_seg = pltpu.make_async_copy(seg, seg_buf.at[1, x], s_loc.at[4])
    hid_send = remote(hid, h_buf.at[tile(x, tok)], s_hid, r_hid, dev(f, z, other))

    def hid_wait():
        remote(hid, h_buf.at[tile(other, tok)], s_hid, r_hid, here).wait_recv()

    def wkv_send(d):
        zz = lax.rem(z + d, nz)
        return remote(
            wkv, wkv_buf.at[tile(z, kvw)], s_wkv.at[d - 1], r_wkv.at[z], dev(f, zz, x)
        )

    def wkv_wait(d):
        zz = lax.rem(z + d, nz)
        remote(
            wkv, wkv_buf.at[tile(zz, kvw)], s_wkv.at[d - 1], r_wkv.at[zz], here
        ).wait_recv()

    def wq_copy(src, j, to_right):
        sems = s_wqr if to_right else s_wql
        return remote(
            src, wq_buf.at[j], sems.at[j], r_wq.at[j],
            dev(f, z + 1 if to_right else z - 1, x),
        )

    def wo_slice(zz, xx, c):
        return wo_buf.at[tile(zz * nx + xx, HD), c * chunk : (c + 1) * chunk]

    def wo_src(j, c, own):
        return wo.at[:, c * chunk : (c + 1) * chunk] if own else wo_slice(j, x, c)

    def wo_copy(j, c, to_right, own=False):
        sems = s_wor if to_right else s_wol
        return remote(
            wo_src(j, c, own), wo_slice(j, x, c), sems.at[j, c], r_wo.at[j * nx + x, c],
            dev(f, z + 1 if to_right else z - 1, x),
        )

    def wo_cross(j, c, own=False):
        return remote(
            wo_src(j, c, own), wo_slice(j, x, c), s_wox.at[j, c], r_wo.at[j * nx + x, c],
            dev(f, z, other),
        )

    def wo_wait(j, xx, c):
        remote(
            wo_slice(j, xx, c), wo_slice(j, xx, c), s_wox.at[j, c], r_wo.at[j * nx + xx, c], here
        ).wait_recv()

    def wo_own(to_right):
        for c in range(WO_CHUNKS):
            wo_copy(z, c, to_right, own=True).start()

    seg_same = remote(seg, seg_buf.at[1, x], s_seg.at[0], r_seg.at[1, x], dev(f, z, other))

    def seg_next(xx):
        return remote(
            seg, seg_buf.at[0, x], s_seg.at[1 + xx], r_seg.at[0, x], dev(f, z + 1, xx)
        )

    barrier = pltpu.get_barrier_semaphore()

    def greet(ff, zz, xx):
        pl.semaphore_signal(
            barrier, inc=1, device_id=dev(ff, zz, xx), device_id_type=pl.DeviceIdType.MESH
        )

    plane = nf * nx
    for step in (1, -1):
        @pl.when((z + step >= 0) & (z + step < nz))
        def _():
            for xx in range(nx):
                for ff in range(nf):
                    greet(ff, z + step, xx)

        for far in range(2, nz):
            @pl.when((z + far * step >= 0) & (z + far * step < nz))
            def _():
                greet(f, z + far * step, x)

    for d in range(1, plane):
        greet(lax.rem(f + d, nf), z, lax.rem(x + d // nf, nx))
    ends = jnp.where(z == 0, 1, 0) + jnp.where(z == nz - 1, 1, 0)
    pl.semaphore_wait(barrier, (3 - ends) * plane - 1 + nz - 3 + ends)

    for d in range(1, nz):
        wkv_send(d).start()

    @pl.when(z < nz - 1)
    def _():
        wq_copy(wq, z, True).start()

    @pl.when(z > 0)
    def _():
        wq_copy(wq, z, False).start()

    @pl.when(z == nz - 2)
    def _():
        wo_own(True)

    @pl.when(z == 1)
    def _():
        wo_own(False)

    hid_send.start()
    seg_same.start()

    @pl.when(z < nz - 1)
    def _():
        for xx in range(nx):
            seg_next(xx).start()

    for copy in (own_h, own_wq, own_wkv, own_wo, own_seg):
        copy.start()

    @pl.when(z == 0)
    def _():
        wo_own(True)
        kv_all[0] = jnp.zeros(kv_all.shape[1:], bf16)
        seg_buf[0] = jnp.full(seg_buf.shape[1:], NEG_POS, jnp.int32)

    @pl.when(z == nz - 1)
    def _():
        wo_own(False)

    def table(row_count, first, lane_index):
        position = (first + lax.broadcasted_iota(jnp.int32, (row_count, HD), 0)).astype(f32)
        frequency = jnp.exp(lane_index.astype(f32) * (-2.0 * math.log(ROPE_BASE) / HD))
        return position * frequency

    lane = lax.broadcasted_iota(jnp.int32, (1, HD), 1)
    half = HD // 2
    quarter = half // nx
    kv_angle = table(sub, z * rows + f * sub, x * quarter + lane % quarter)
    is_key = lane < half
    kv_cos = jnp.where(is_key, jnp.cos(kv_angle), 1.0)
    kv_sin = jnp.where(is_key, jnp.sin(kv_angle), 0.0)
    kv_sin = jnp.where(lane < quarter, -kv_sin, kv_sin)
    q_angle = table(rows, z * rows, lane % half)
    q_sine = jnp.sin(q_angle)
    q_cos[...] = jnp.cos(q_angle)
    q_sin[...] = jnp.where(lane < half, -q_sine, q_sine)

    def wq_step(d):
        @pl.when(z >= d)
        def _():
            j = z - d
            wq_copy(wq_buf.at[j], j, True).wait_recv()

            @pl.when(z < nz - 1)
            def _():
                wq_copy(wq_buf.at[j], j, True).start()

                @pl.when((z == d) & (z != nz - 2))
                def _():
                    wo_own(True)

        @pl.when(z + d < nz)
        def _():
            j = z + d
            wq_copy(wq_buf.at[j], j, False).wait_recv()

            @pl.when(z > 0)
            def _():
                wq_copy(wq_buf.at[j], j, False).start()

                @pl.when((z + d == nz - 1) & (z != 1))
                def _():
                    wo_own(False)

    def q_send(j):
        return remote(q_part.at[j], q_recv.at[f], s_q.at[j], r_q.at[f], (j, s))

    def q_project(j):
        q_part[j] = jnp.dot(h_buf[...], wq_buf[j], preferred_element_type=f32)

        @pl.when(j != f)
        def _():
            q_send(j).start()

    def q_step(d):
        @pl.when(z >= d)
        def _():
            q_project(z - d)

        @pl.when(z + d < nz)
        def _():
            q_project(z + d)

    def wo_end(d, c):
        for end, j in ((0, d), (nz - 1, nz - 1 - d)):
            @pl.when(z == end)
            def _():
                wo_wait(j, x, c)
                wo_cross(j, c).start()

    wq_step(1)
    own_h.wait()
    own_wq.wait()
    own_wkv.wait()
    hid_wait()
    for c in range(WO_CHUNKS):
        wo_cross(z, c, own=True).start()
    for d in range(1, nz):
        wkv_wait(d)
    kv_part[...] = lax.dot_general(
        h_buf[...], wkv_buf[...], (((1,), (1,)), ((), ())), preferred_element_type=f32
    )

    def kvp_send(d):
        ff = lax.rem(f + d, nf)
        return remote(
            kv_part.at[tile(ff, sub)], kv_recv.at[f], s_kvp.at[d - 1], r_kvp.at[f], (ff, s)
        )

    def kvp_wait(d):
        ff = lax.rem(f + d, nf)
        remote(
            kv_part.at[tile(ff, sub)], kv_recv.at[ff], s_kvp.at[d - 1], r_kvp.at[ff], here
        ).wait_recv()

    for d in range(1, nf):
        kvp_send(d).start()
    inner = (z > 0) & (z < nz - 1)

    @pl.when(inner)
    def _():
        wq_step(2)

    q_project(z)
    q_step(1)
    total = kv_part[tile(f, sub), :]
    for d in range(1, nf):
        kvp_wait(d)
        total = total + kv_recv[lax.rem(f + d, nf)]
    partner = jnp.where(
        lane < quarter, pltpu.roll(total, HD - quarter, 1), pltpu.roll(total, quarter, 1)
    )
    kv_piece[...] = (total * kv_cos + partner * kv_sin).astype(bf16)
    piece_rows = tile(f, sub)
    own_piece = pltpu.make_async_copy(kv_piece, kv_all.at[1, x, piece_rows], s_loc.at[5])
    own_piece.start()

    def kv_send(plane, dx, d):
        ff, xx = lax.rem(f + d, nf), lax.rem(x + dx, nx)
        slot = kv_all.at[plane, x, piece_rows]
        return remote(
            kv_piece if plane else slot, slot,
            s_kv.at[plane, dx, d], r_kv.at[plane, x, f], dev(ff, z, xx),
        )

    def kv_next():
        return remote(
            kv_piece, kv_all.at[0, x, piece_rows],
            s_kv.at[0, 0, 0], r_kv.at[0, x, f], dev(f, z + 1, x),
        )

    def kv_wait(plane, dx, d):
        ff, xx = lax.rem(f + d, nf), lax.rem(x + dx, nx)
        remote(
            kv_piece, kv_all.at[plane, xx, tile(ff, sub)],
            s_kv.at[plane, dx, d], r_kv.at[plane, xx, ff], here,
        ).wait_recv()

    pairs = [(dx, d) for dx in range(nx) for d in range(nf)]
    for pair in pairs[1:]:
        kv_send(1, *pair).start()

    @pl.when(z < nz - 1)
    def _():
        kv_next().start()

    for c in range(WO_CHUNKS):
        wo_end(1, c)

    @pl.when(jnp.logical_not(inner))
    def _():
        wq_step(2)

    q_step(2)

    @pl.when(z > 0)
    def _():
        kv_wait(0, 0, 0)
        for pair in pairs[1:]:
            kv_send(0, *pair).start()

    for d in range(3, nz):
        wq_step(d)
        q_step(d)

    def wo_side(j, to_right):
        for c in range(WO_CHUNKS):
            wo_wait(j, x, c)
            wo_copy(j, c, to_right).start()
            wo_cross(j, c).start()

    def wo_mid(d):
        @pl.when((z >= d) & (z < nz - 1))
        def _():
            wo_side(z - d, True)

        @pl.when((z + d < nz) & (z > 0))
        def _():
            wo_side(z + d, False)

    for d in range(1, nz - 1):
        wo_mid(d)

    q_total = q_part[f]
    for d in range(1, nf):
        ff = lax.rem(f + d, nf)
        remote(q_part.at[0], q_recv.at[ff], s_q.at[0], r_q.at[ff], here).wait_recv()
        q_total = q_total + q_recv[ff]
    q_turned = q_total * q_cos[...] + pltpu.roll(q_total, half, 1) * q_sin[...]
    q_head = q_turned.astype(bf16).astype(f32)
    quarters = []
    for xx in range(nx):
        low = q_head if xx == 0 else pltpu.roll(q_head, HD - xx * quarter, 1)
        high = pltpu.roll(q_head, (HD - half - xx * quarter + quarter) % HD, 1)
        picked = jnp.where(lane < quarter, low, jnp.where(lane < half, high, 0.0))
        quarters.append(picked.astype(bf16))

    own_seg.wait()
    seg_wait = lambda plane, xx: remote(
        seg, seg_buf.at[plane, xx], s_seg.at[0], r_seg.at[plane, xx], here
    ).wait_recv()
    seg_wait(1, other)
    own_piece.wait()
    for pair in pairs[1:]:
        kv_wait(1, *pair)

    @pl.when(z > 0)
    def _():
        for xx in range(nx):
            seg_wait(0, xx)
        for pair in pairs[1:]:
            kv_wait(0, *pair)

    key_seg = jnp.concatenate(
        [seg_buf[plane, xx] for plane in range(2) for xx in range(nx)], axis=1
    )
    own_seg_row = key_seg[:, rows:]
    seg_column = jnp.transpose(jnp.broadcast_to(own_seg_row, (HD, rows)))[:, :1]
    key_pos = lax.broadcasted_iota(jnp.int32, (1, 2 * rows), 1) - rows
    keys = [
        jnp.concatenate([kv_all[0, xx], kv_all[1, xx]], axis=0) for xx in range(nx)
    ]
    step_rows = rows // nf
    for b in range(nf):
        span = slice(b * step_rows, (b + 1) * step_rows)
        query_pos = b * step_rows + lax.broadcasted_iota(jnp.int32, (step_rows, 1), 0)
        score = None
        for xx in range(nx):
            term = lax.dot_general(
                quarters[xx][span], keys[xx], (((1,), (1,)), ((), ())),
                preferred_element_type=f32,
            )
            score = term if score is None else score + term
        allowed = (key_pos <= query_pos) & (key_seg == seg_column[span])
        masked = jnp.where(allowed, score * HD ** (-0.5), NEG_FILL)
        row_max = jnp.max(masked, axis=1, keepdims=True)
        weight = jnp.where(allowed, jnp.exp(masked - row_max), 0.0)
        row_total = jnp.sum(weight, axis=1, keepdims=True)
        rounded = weight.astype(bf16)
        product = [
            jnp.dot(rounded, keys[xx], preferred_element_type=f32) for xx in range(nx)
        ]
        mixed = None
        for xx in reversed(range(nx)):
            low = pltpu.roll(product[xx], (half + xx * quarter) % HD, 1)
            high = pltpu.roll(product[xx], (HD - (nx - 1 - xx) * quarter) % HD, 1)
            lane_block = lane // quarter
            value = jnp.where(lane_block < nx, low, high)
            mixed = value if mixed is None else jnp.where(lane_block % nx == xx, value, mixed)
        mix_own[span, :] = (mixed / row_total).astype(bf16)

    head = f * nx + x

    def mix_send(dx, d):
        ff, xx = lax.rem(f + d, nf), lax.rem(x + dx, nx)
        return remote(
            mix_own.at[tile(xx, tok)], mix_buf.at[:, tile(head, HD)],
            s_mix.at[dx, d], r_mix.at[x, f], dev(ff, z, xx),
        )

    def mix_wait(dx, d):
        ff, xx = lax.rem(f + d, nf), lax.rem(x + dx, nx)
        remote(
            mix_own.at[tile(x, tok)], mix_buf.at[:, tile(ff * nx + xx, HD)],
            s_mix.at[dx, d], r_mix.at[xx, ff], here,
        ).wait_recv()

    for pair in pairs[1:]:
        mix_send(*pair).start()
    own_mix = pltpu.make_async_copy(
        mix_own.at[tile(x, tok)], mix_buf.at[:, tile(head, HD)], s_loc.at[6]
    )
    own_mix.start()
    for d in range(2, nz - 1):
        for c in range(WO_CHUNKS):
            wo_end(d, c)
    own_mix.wait()
    own_wo.wait()
    for pair in pairs[1:]:
        mix_wait(*pair)
    wo_end(nz - 1, 0)
    for c in range(WO_CHUNKS):
        if c + 1 < WO_CHUNKS:
            wo_end(nz - 1, c + 1)
        for j in range(nz):
            wo_wait(j, other, c)
        out[:, c * chunk : (c + 1) * chunk] = jnp.dot(
            mix_buf[...], wo_buf[:, c * chunk : (c + 1) * chunk], preferred_element_type=f32
        ).astype(bf16)

    hid_send.wait_send()
    seg_same.wait_send()
    for d in range(1, nz):
        wkv_send(d).wait_send()
    for d in range(1, nf):
        kvp_send(d).wait_send()
        q_send(lax.rem(f + d, nf)).wait_send()
    for pair in pairs[1:]:
        kv_send(1, *pair).wait_send()
        mix_send(*pair).wait_send()

    @pl.when(z < nz - 1)
    def _():
        for xx in range(nx):
            seg_next(xx).wait_send()
        kv_next().wait_send()

    @pl.when(z > 0)
    def _():
        for pair in pairs[1:]:
            kv_send(0, *pair).wait_send()

    for j in range(nz):
        for c in range(WO_CHUNKS):
            wo_cross(j, c).wait_send()

        @pl.when((z < nz - 1) & (z >= j))
        def _():
            wq_copy(wq, j, True).wait_send()
            for c in range(WO_CHUNKS):
                wo_copy(j, c, True).wait_send()

        @pl.when((z > 0) & (z <= j))
        def _():
            wq_copy(wq, j, False).wait_send()
            for c in range(WO_CHUNKS):
                wo_copy(j, c, False).wait_send()


def fused_on_device(nf, nz, nx, hidden, w_query, w_keyvalue, w_output, segment_ids):
    tok, kdim = hidden.shape
    cols = w_output.shape[1]
    rows = tok * nx
    sub = rows // nf
    kvw = w_keyvalue.shape[1]
    f32, bf16 = jnp.float32, jnp.bfloat16
    dma = pltpu.SemaphoreType.DMA
    vmem = pl.BlockSpec(memory_space=pltpu.VMEM)
    scratch = [
        pltpu.VMEM((rows, kdim), bf16),
        pltpu.VMEM((nz, kdim, HD), bf16),
        pltpu.VMEM((nz * kvw, kdim), bf16),
        pltpu.VMEM((nz * nx * HD, cols), bf16),
        pltpu.VMEM((2, nx, 1, tok), jnp.int32),
        pltpu.VMEM((nz, rows, HD), f32),
        pltpu.VMEM((nf, rows, HD), f32),
        pltpu.VMEM((rows, nz * kvw), f32),
        pltpu.VMEM((nf, sub, nz * kvw), f32),
        pltpu.VMEM((sub, HD), bf16),
        pltpu.VMEM((2, nx, rows, HD), bf16),
        pltpu.VMEM((rows, HD), bf16),
        pltpu.VMEM((tok, nz * nx * HD), bf16),
        pltpu.VMEM((rows, HD), f32),
        pltpu.VMEM((rows, HD), f32),
        dma((7,)), dma, dma, dma((1 + nx,)), dma((2, nx)),
        dma((nz,)), dma((nz,)), dma((nz,)), dma((nz,)), dma((nz,)),
        dma((nz,)), dma((nf,)), dma((nf,)), dma((nf,)),
        dma((2, nx, nf)), dma((2, nx, nf)),
        dma((nz, WO_CHUNKS)), dma((nz, WO_CHUNKS)), dma((nz, WO_CHUNKS)),
        dma((nz * nx, WO_CHUNKS)), dma((nx, nf)), dma((nx, nf)),
    ]
    return pl.pallas_call(
        functools.partial(fused_kernel, nf, nz, nx),
        out_shape=jax.ShapeDtypeStruct((tok, cols), bf16),
        in_specs=[vmem] * 5,
        out_specs=vmem,
        scratch_shapes=scratch,
        name="fused_sublayer",
        compiler_params=pltpu.CompilerParams(
            collective_id=0, has_side_effects=True, vmem_limit_bytes=60 * 1024 * 1024
        ),
    )(hidden, w_query, w_keyvalue.T, w_output, segment_ids.reshape(1, tok))


def solution(mesh):
    in_specs = (P("sp", "fsdp"), P("fsdp", "sp"), P("fsdp", "sp"), P("sp", "fsdp"), P("sp"))
    out_specs = P("sp", "fsdp")
    nf, sp = mesh.shape["fsdp"], mesh.shape["sp"]
    if sp == GROUP and sp == 2 * nf:
        body = functools.partial(fused_on_device, nf, nf, sp // nf)
    else:
        body = on_device
    return jax.shard_map(
        body, mesh=mesh, in_specs=in_specs, out_specs=out_specs, check_vma=False
    )
```

profile of v0, /device:TPU:24, one launch (start us, length us, event | category | flops | bytes accessed | tf_op | source)
XLA Modules:
  0.0 104.9 jit_solution(8740777669122016673)
XLA Ops:
  0.0 102.6 %fused_sublayer.1 = bf16[256,2048]{1,0:T(8,128)(2,1)} custom-call(bf16[256,2048]{1,0:T(8,128)(2,1)} %hid.1, bf16[2048,128]{1,0:T(8,128)(2,1)} %wq.1, bf16[32,2048]{1,0:T(8,128)(2,1)} %bitcast.2, bf16[128,2048]{1,0:T(8,128)(2,1)} %wo.1, s32[1,256]{1,0:T(1,128)} %bitcast.3), custom_call_target="tpu_custom_call" | custom-call | tf_op jit(solution)/shard_map/fused_sublayer/pallas_call | solution.py:658
  102.6 2.3 %copy.7 = bf16[256,2048]{1,0:T(8,128)(2,1)} copy(bf16[256,2048]{1,0:T(8,128)(2,1)} %fused_sublayer.1) | data formatting | bytes 2097152
where the time goes:
time: 105 us
  Pallas kernels  103 us (98%)
  local copies, waits for them, and re-layouts  2.3 us (2%)
    pallas_call x1, Pallas kernels, fused_on_device(): pl.pallas_call(functools.partial(fused_kernel, nf, nz, nx), out_shape=jax...  103 us
    unnamed x1, local copies, waits for them, and re-layouts  2.3 us

commit v1 on v0

--- a/solution.py
+++ b/solution.py
@@ -137,8 +137,10 @@
     nf, nz, nx, hid, wq, wkv, wo, seg, out,
     h_buf, wq_buf, wkv_buf, wo_buf, seg_buf,
     q_part, q_recv, kv_part, kv_recv, kv_piece, kv_all, mix_own, mix_buf, q_cos, q_sin,
-    s_loc, s_hid, r_hid, s_seg, r_seg, s_wkv, r_wkv, s_wqr, s_wql, r_wq,
-    s_q, r_q, s_kvp, r_kvp, s_kv, r_kv, s_wor, s_wol, s_wox, r_wo, s_mix, r_mix,
+    out_buf, out_away,
+    s_loc, s_hid, r_hid, s_seg, r_seg, s_wkv, r_wkv, s_wq, r_wq,
+    s_q, r_q, s_kvp, r_kvp, s_kv, r_kv, s_wo, r_wo, s_wox, r_wox, s_mix, r_mix,
+    s_out, r_out, s_res,
 ):
     f = lax.axis_index("fsdp")
     s = lax.axis_index("sp")
@@ -148,8 +150,16 @@
     sub = rows // nf
     kvw = wkv.shape[0]
     other = 1 - x
-    chunk = wo.shape[1] // WO_CHUNKS
+    half_cols = wo.shape[1] // nx
+    chunk = half_cols // WO_CHUNKS
     f32, bf16 = jnp.float32, jnp.bfloat16
+    is_end = (z == 0) | (z == nz - 1)
+    is_inner = jnp.logical_not(is_end)
+    low = z < nz // 2
+    e = jnp.where(low, 0, nz - 1)
+    n = jnp.where(low, 1, nz - 2)
+    m = nz - 1 - n
+    e2 = nz - 1 - e
 
     def dev(ff, zz, xx):
         return (ff, zz * nx + xx)
@@ -164,68 +174,82 @@
         return pl.ds(pl.multiple_of(ref * count, count), count)
 
     here = (f, s)
+    pending = {"all": [], "end": [], "inner": []}
+
+    def go(kind, make):
+        make().start()
+        pending[kind].append(make)
+
+    def cols(c):
+        return slice(c * chunk, (c + 1) * chunk)
+
     own_h = pltpu.make_async_copy(hid, h_buf.at[tile(x, tok)], s_loc.at[0])
     own_wq = pltpu.make_async_copy(wq, wq_buf.at[z], s_loc.at[1])
     own_wkv = pltpu.make_async_copy(wkv, wkv_buf.at[tile(z, kvw)], s_loc.at[2])
-    own_wo = pltpu.make_async_copy(wo, wo_buf.at[tile(s, HD)], s_loc.at[3])
-    own_seg = pltpu.make_async_copy(seg, seg_buf.at[1, x], s_loc.at[4])
-    hid_send = remote(hid, h_buf.at[tile(x, tok)], s_hid, r_hid, dev(f, z, other))
+    own_wo = [
+        pltpu.make_async_copy(
+            wo.at[:, h * half_cols : (h + 1) * half_cols],
+            wo_buf.at[h, tile(s, HD)], s_loc.at[3 + h],
+        )
+        for h in range(nx)
+    ]
+    own_seg = pltpu.make_async_copy(seg, seg_buf.at[1, x], s_loc.at[5])
+    for copy in (own_wkv, own_wq, own_h, *own_wo, own_seg):
+        copy.start()
+
+    def hid_send():
+        return remote(
+            h_buf.at[tile(x, tok)], h_buf.at[tile(x, tok)], s_hid, r_hid, dev(f, z, other)
+        )
 
     def hid_wait():
-        remote(hid, h_buf.at[tile(other, tok)], s_hid, r_hid, here).wait_recv()
-
-    def wkv_send(d):
-        zz = lax.rem(z + d, nz)
-        return remote(
-            wkv, wkv_buf.at[tile(z, kvw)], s_wkv.at[d - 1], r_wkv.at[z], dev(f, zz, x)
-        )
-
-    def wkv_wait(d):
-        zz = lax.rem(z + d, nz)
         remote(
-            wkv, wkv_buf.at[tile(zz, kvw)], s_wkv.at[d - 1], r_wkv.at[zz], here
+            h_buf.at[tile(other, tok)], h_buf.at[tile(other, tok)], s_hid, r_hid, here
         ).wait_recv()
 
-    def wq_copy(src, j, to_right):
-        sems = s_wqr if to_right else s_wql
-        return remote(
-            src, wq_buf.at[j], sems.at[j], r_wq.at[j],
-            dev(f, z + 1 if to_right else z - 1, x),
-        )
-
-    def wo_slice(zz, xx, c):
-        return wo_buf.at[tile(zz * nx + xx, HD), c * chunk : (c + 1) * chunk]
-
-    def wo_src(j, c, own):
-        return wo.at[:, c * chunk : (c + 1) * chunk] if own else wo_slice(j, x, c)
-
-    def wo_copy(j, c, to_right, own=False):
-        sems = s_wor if to_right else s_wol
-        return remote(
-            wo_src(j, c, own), wo_slice(j, x, c), sems.at[j, c], r_wo.at[j * nx + x, c],
-            dev(f, z + 1 if to_right else z - 1, x),
-        )
-
-    def wo_cross(j, c, own=False):
-        return remote(
-            wo_src(j, c, own), wo_slice(j, x, c), s_wox.at[j, c], r_wo.at[j * nx + x, c],
-            dev(f, z, other),
-        )
+    def wkv_z(j, d, target):
+        ref = wkv_buf.at[tile(j, kvw)]
+        return remote(ref, ref, s_wkv.at[d, j], r_wkv.at[j], dev(f, target, x))
+
+    def wkv_wait(j):
+        wkv_z(j, 0, z).wait_recv()
+
+    def wq_z(j, d, target):
+        ref = wq_buf.at[j]
+        return remote(ref, ref, s_wq.at[d, j], r_wq.at[j], dev(f, target, x))
+
+    def wq_wait(j):
+        wq_z(j, 0, z).wait_recv()
+
+    def wo_unit(h, j, xx, c):
+        return wo_buf.at[h, tile(j * nx + xx, HD), cols(c)]
+
+    def wo_z(j, xx, c, d, target):
+        ref = wo_unit(x, j, xx, c)
+        return remote(ref, ref, s_wo.at[d, j, xx, c], r_wo.at[j, xx, c], dev(f, target, x))
+
+    def wo_pair(c):
+        ref = wo_unit(other, z, x, c)
+        return remote(ref, ref, s_wox.at[nz, x, c], r_wo.at[z, x, c], dev(f, z, other))
 
     def wo_wait(j, xx, c):
-        remote(
-            wo_slice(j, xx, c), wo_slice(j, xx, c), s_wox.at[j, c], r_wo.at[j * nx + xx, c], here
-        ).wait_recv()
-
-    def wo_own(to_right):
-        for c in range(WO_CHUNKS):
-            wo_copy(z, c, to_right, own=True).start()
-
-    seg_same = remote(seg, seg_buf.at[1, x], s_seg.at[0], r_seg.at[1, x], dev(f, z, other))
+        ref = wo_unit(x, j, xx, c)
+        remote(ref, ref, s_wox.at[0, 0, c], r_wo.at[j, xx, c], here).wait_recv()
+
+    def wo_cross(j, xx, c):
+        ref = wo_unit(x, j, xx, c)
+        return remote(ref, ref, s_wox.at[j, xx, c], r_wox.at[j, xx, c], dev(f, z, other))
+
+    def wox_wait(j, xx, c):
+        ref = wo_unit(other, j, xx, c)
+        remote(ref, ref, s_wox.at[0, 0, c], r_wox.at[j, xx, c], here).wait_recv()
+
+    def seg_same():
+        return remote(seg_buf.at[1, x], seg_buf.at[1, x], s_seg.at[0], r_seg.at[1, x], dev(f, z, other))
 
     def seg_next(xx):
         return remote(
-            seg, seg_buf.at[0, x], s_seg.at[1 + xx], r_seg.at[0, x], dev(f, z + 1, xx)
+            seg_buf.at[1, x], seg_buf.at[0, x], s_seg.at[1 + xx], r_seg.at[0, x], dev(f, z + 1, xx)
         )
 
     barrier = pltpu.get_barrier_semaphore()
@@ -240,58 +264,52 @@
         @pl.when((z + step >= 0) & (z + step < nz))
         def _():
             for xx in range(nx):
-                for ff in range(nf):
-                    greet(ff, z + step, xx)
-
-        for far in range(2, nz):
-            @pl.when((z + far * step >= 0) & (z + far * step < nz))
-            def _():
-                greet(f, z + far * step, x)
+                greet(f, z + step, xx)
 
     for d in range(1, plane):
         greet(lax.rem(f + d, nf), z, lax.rem(x + d // nf, nx))
-    ends = jnp.where(z == 0, 1, 0) + jnp.where(z == nz - 1, 1, 0)
-    pl.semaphore_wait(barrier, (3 - ends) * plane - 1 + nz - 3 + ends)
-
-    for d in range(1, nz):
-        wkv_send(d).start()
-
-    @pl.when(z < nz - 1)
-    def _():
-        wq_copy(wq, z, True).start()
-
-    @pl.when(z > 0)
-    def _():
-        wq_copy(wq, z, False).start()
-
-    @pl.when(z == nz - 2)
-    def _():
-        wo_own(True)
-
-    @pl.when(z == 1)
-    def _():
-        wo_own(False)
-
-    hid_send.start()
-    seg_same.start()
+    pl.semaphore_wait(barrier, plane - 1 + jnp.where(is_end, nx, 2 * nx))
+
+    own_wkv.wait()
+    own_wq.wait()
+
+    @pl.when(is_end)
+    def _():
+        go("end", lambda: wkv_z(z, 1, n))
+        go("end", lambda: wq_z(z, 1, n))
+
+    @pl.when(is_inner)
+    def _():
+        for d, target in ((0, e), (1, m)):
+            go("inner", lambda d=d, target=target: wkv_z(z, d, target))
+            go("inner", lambda d=d, target=target: wq_z(z, d, target))
+
+    own_h.wait()
+    go("all", hid_send)
+    own_seg.wait()
+    go("all", seg_same)
 
     @pl.when(z < nz - 1)
     def _():
         for xx in range(nx):
             seg_next(xx).start()
 
-    for copy in (own_h, own_wq, own_wkv, own_wo, own_seg):
-        copy.start()
+    for copy in own_wo:
+        copy.wait()
+    for c in range(WO_CHUNKS):
+        go("all", lambda c=c: wo_pair(c))
+
+    @pl.when(is_end)
+    def _():
+        for c in range(WO_CHUNKS):
+            go("end", lambda c=c: wo_z(z, x, c, 1, n))
+        for c in range(WO_CHUNKS):
+            go("end", lambda c=c: wo_cross(z, x, c))
 
     @pl.when(z == 0)
     def _():
-        wo_own(True)
         kv_all[0] = jnp.zeros(kv_all.shape[1:], bf16)
         seg_buf[0] = jnp.full(seg_buf.shape[1:], NEG_POS, jnp.int32)
-
-    @pl.when(z == nz - 1)
-    def _():
-        wo_own(False)
 
     def table(row_count, first, lane_index):
         position = (first + lax.broadcasted_iota(jnp.int32, (row_count, HD), 0)).astype(f32)
@@ -311,33 +329,6 @@
     q_cos[...] = jnp.cos(q_angle)
     q_sin[...] = jnp.where(lane < half, -q_sine, q_sine)
 
-    def wq_step(d):
-        @pl.when(z >= d)
-        def _():
-            j = z - d
-            wq_copy(wq_buf.at[j], j, True).wait_recv()
-
-            @pl.when(z < nz - 1)
-            def _():
-                wq_copy(wq_buf.at[j], j, True).start()
-
-                @pl.when((z == d) & (z != nz - 2))
-                def _():
-                    wo_own(True)
-
-        @pl.when(z + d < nz)
-        def _():
-            j = z + d
-            wq_copy(wq_buf.at[j], j, False).wait_recv()
-
-            @pl.when(z > 0)
-            def _():
-                wq_copy(wq_buf.at[j], j, False).start()
-
-                @pl.when((z + d == nz - 1) & (z != 1))
-                def _():
-                    wo_own(False)
-
     def q_send(j):
         return remote(q_part.at[j], q_recv.at[f], s_q.at[j], r_q.at[f], (j, s))
 
@@ -348,31 +339,43 @@
         def _():
             q_send(j).start()
 
-    def q_step(d):
-        @pl.when(z >= d)
-        def _():
-            q_project(z - d)
-
-        @pl.when(z + d < nz)
-        def _():
-            q_project(z + d)
-
-    def wo_end(d, c):
-        for end, j in ((0, d), (nz - 1, nz - 1 - d)):
-            @pl.when(z == end)
-            def _():
-                wo_wait(j, x, c)
-                wo_cross(j, c).start()
-
-    wq_step(1)
-    own_h.wait()
-    own_wq.wait()
-    own_wkv.wait()
+    @pl.when(is_inner)
+    def _():
+        wkv_wait(e)
+        go("inner", lambda: wkv_z(e, 1, m))
+        wkv_wait(m)
+        go("inner", lambda: wkv_z(m, 0, e))
+        wq_wait(e)
+        go("inner", lambda: wq_z(e, 1, m))
+        for c in range(WO_CHUNKS):
+            go("inner", lambda c=c: wo_z(z, x, c, 1, m))
+        wq_wait(m)
+        go("inner", lambda: wq_z(m, 0, e))
+        wkv_wait(e2)
+        go("inner", lambda: wkv_z(e2, 0, e))
+
     hid_wait()
-    for c in range(WO_CHUNKS):
-        wo_cross(z, c, own=True).start()
-    for d in range(1, nz):
-        wkv_wait(d)
+    q_project(z)
+
+    @pl.when(is_inner)
+    def _():
+        q_project(e)
+        q_project(m)
+        wq_wait(e2)
+        go("inner", lambda: wq_z(e2, 0, e))
+
+    @pl.when(is_end)
+    def _():
+        wq_wait(n)
+        q_project(n)
+        for c in range(WO_CHUNKS):
+            wo_wait(z, other, c)
+            go("end", lambda c=c: wo_z(z, other, c, 1, n))
+        wq_wait(m)
+        q_project(m)
+        for j in (n, m, e2):
+            wkv_wait(j)
+
     kv_part[...] = lax.dot_general(
         h_buf[...], wkv_buf[...], (((1,), (1,)), ((), ())), preferred_element_type=f32
     )
@@ -390,15 +393,19 @@
         ).wait_recv()
 
     for d in range(1, nf):
-        kvp_send(d).start()
-    inner = (z > 0) & (z < nz - 1)
-
-    @pl.when(inner)
-    def _():
-        wq_step(2)
-
-    q_project(z)
-    q_step(1)
+        go("all", lambda d=d: kvp_send(d))
+
+    @pl.when(is_inner)
+    def _():
+        q_project(e2)
+        for c in range(WO_CHUNKS):
+            go("inner", lambda c=c: wo_z(z, x, c, 0, e))
+        for c in range(WO_CHUNKS):
+            wo_wait(z, other, c)
+            go("inner", lambda c=c: wo_z(z, other, c, 1, m))
+        for c in range(WO_CHUNKS):
+            go("inner", lambda c=c: wo_z(z, other, c, 0, e))
+
     total = kv_part[tile(f, sub), :]
     for d in range(1, nf):
         kvp_wait(d)
@@ -408,7 +415,7 @@
     )
     kv_piece[...] = (total * kv_cos + partner * kv_sin).astype(bf16)
     piece_rows = tile(f, sub)
-    own_piece = pltpu.make_async_copy(kv_piece, kv_all.at[1, x, piece_rows], s_loc.at[5])
+    own_piece = pltpu.make_async_copy(kv_piece, kv_all.at[1, x, piece_rows], s_loc.at[6])
     own_piece.start()
 
     def kv_send(plane, dx, d):
@@ -434,20 +441,18 @@
 
     pairs = [(dx, d) for dx in range(nx) for d in range(nf)]
     for pair in pairs[1:]:
-        kv_send(1, *pair).start()
+        go("all", lambda pair=pair: kv_send(1, *pair))
 
     @pl.when(z < nz - 1)
     def _():
         kv_next().start()
 
-    for c in range(WO_CHUNKS):
-        wo_end(1, c)
-
-    @pl.when(jnp.logical_not(inner))
-    def _():
-        wq_step(2)
-
-    q_step(2)
+    @pl.when(is_inner)
+    def _():
+        for xx in range(nx):
+            for c in range(WO_CHUNKS):
+                wo_wait(e, xx, c)
+                go("inner", lambda xx=xx, c=c: wo_z(e, xx, c, 1, m))
 
     @pl.when(z > 0)
     def _():
@@ -455,27 +460,10 @@
         for pair in pairs[1:]:
             kv_send(0, *pair).start()
 
-    for d in range(3, nz):
-        wq_step(d)
-        q_step(d)
-
-    def wo_side(j, to_right):
-        for c in range(WO_CHUNKS):
-            wo_wait(j, x, c)
-            wo_copy(j, c, to_right).start()
-            wo_cross(j, c).start()
-
-    def wo_mid(d):
-        @pl.when((z >= d) & (z < nz - 1))
-        def _():
-            wo_side(z - d, True)
-
-        @pl.when((z + d < nz) & (z > 0))
-        def _():
-            wo_side(z + d, False)
-
-    for d in range(1, nz - 1):
-        wo_mid(d)
+    @pl.when(is_end)
+    def _():
+        wq_wait(e2)
+        q_project(e2)
 
     q_total = q_part[f]
     for d in range(1, nf):
@@ -486,14 +474,13 @@
     q_head = q_turned.astype(bf16).astype(f32)
     quarters = []
     for xx in range(nx):
-        low = q_head if xx == 0 else pltpu.roll(q_head, HD - xx * quarter, 1)
-        high = pltpu.roll(q_head, (HD - half - xx * quarter + quarter) % HD, 1)
-        picked = jnp.where(lane < quarter, low, jnp.where(lane < half, high, 0.0))
+        first = q_head if xx == 0 else pltpu.roll(q_head, HD - xx * quarter, 1)
+        second = pltpu.roll(q_head, (HD - half - xx * quarter + quarter) % HD, 1)
+        picked = jnp.where(lane < quarter, first, jnp.where(lane < half, second, 0.0))
         quarters.append(picked.astype(bf16))
 
-    own_seg.wait()
     seg_wait = lambda plane, xx: remote(
-        seg, seg_buf.at[plane, xx], s_seg.at[0], r_seg.at[plane, xx], here
+        seg_buf.at[plane, xx], seg_buf.at[plane, xx], s_seg.at[0], r_seg.at[plane, xx], here
     ).wait_recv()
     seg_wait(1, other)
     own_piece.wait()
@@ -538,62 +525,123 @@
         ]
         mixed = None
         for xx in reversed(range(nx)):
-            low = pltpu.roll(product[xx], (half + xx * quarter) % HD, 1)
-            high = pltpu.roll(product[xx], (HD - (nx - 1 - xx) * quarter) % HD, 1)
+            first = pltpu.roll(product[xx], (half + xx * quarter) % HD, 1)
+            second = pltpu.roll(product[xx], (HD - (nx - 1 - xx) * quarter) % HD, 1)
             lane_block = lane // quarter
-            value = jnp.where(lane_block < nx, low, high)
+            value = jnp.where(lane_block < nx, first, second)
             mixed = value if mixed is None else jnp.where(lane_block % nx == xx, value, mixed)
         mix_own[span, :] = (mixed / row_total).astype(bf16)
 
     head = f * nx + x
 
-    def mix_send(dx, d):
+    def mix_part(dx, d):
         ff, xx = lax.rem(f + d, nf), lax.rem(x + dx, nx)
         return remote(
-            mix_own.at[tile(xx, tok)], mix_buf.at[:, tile(head, HD)],
+            mix_own.at[tile(xx, tok)], mix_buf.at[0:tok, tile(head, HD)],
             s_mix.at[dx, d], r_mix.at[x, f], dev(ff, z, xx),
         )
 
-    def mix_wait(dx, d):
+    def mix_whole(dx, d):
         ff, xx = lax.rem(f + d, nf), lax.rem(x + dx, nx)
+        return remote(
+            mix_own, mix_buf.at[:, tile(head, HD)],
+            s_mix.at[dx, d], r_mix.at[x, f], dev(ff, z, xx),
+        )
+
+    def mix_wait(dx, d, count):
+        ff, xx = lax.rem(f + d, nf), lax.rem(x + dx, nx)
+        ref = mix_buf.at[0:count, tile(ff * nx + xx, HD)]
         remote(
-            mix_own.at[tile(x, tok)], mix_buf.at[:, tile(ff * nx + xx, HD)],
-            s_mix.at[dx, d], r_mix.at[xx, ff], here,
+            ref, ref, s_mix.at[dx, d], r_mix.at[xx, ff], here,
         ).wait_recv()
 
-    for pair in pairs[1:]:
-        mix_send(*pair).start()
-    own_mix = pltpu.make_async_copy(
-        mix_own.at[tile(x, tok)], mix_buf.at[:, tile(head, HD)], s_loc.at[6]
-    )
-    own_mix.start()
-    for d in range(2, nz - 1):
-        for c in range(WO_CHUNKS):
-            wo_end(d, c)
-    own_mix.wait()
-    own_wo.wait()
-    for pair in pairs[1:]:
-        mix_wait(*pair)
-    wo_end(nz - 1, 0)
-    for c in range(WO_CHUNKS):
-        if c + 1 < WO_CHUNKS:
-            wo_end(nz - 1, c + 1)
-        for j in range(nz):
-            wo_wait(j, other, c)
-        out[:, c * chunk : (c + 1) * chunk] = jnp.dot(
-            mix_buf[...], wo_buf[:, c * chunk : (c + 1) * chunk], preferred_element_type=f32
-        ).astype(bf16)
-
-    hid_send.wait_send()
-    seg_same.wait_send()
-    for d in range(1, nz):
-        wkv_send(d).wait_send()
+    far = [pair for pair in pairs[1:] if pair[0]] + [pair for pair in pairs[1:] if not pair[0]]
+
+    @pl.when(is_end)
+    def _():
+        for pair in far:
+            go("end", lambda pair=pair: mix_part(*pair))
+        mix_buf[0:tok, tile(head, HD)] = mix_own[tile(x, tok), :]
+
+    @pl.when(is_inner)
+    def _():
+        for pair in far:
+            go("inner", lambda pair=pair: mix_whole(*pair))
+        mix_buf[:, tile(head, HD)] = mix_own[...]
+
+    def result(h, c):
+        where = pl.ds(pl.multiple_of(h * half_cols + c * chunk, chunk), chunk)
+        return pltpu.make_async_copy(out_buf.at[h, :, cols(c)], out.at[:, where], s_res.at[h, c])
+
+    @pl.when(is_inner)
+    def _():
+        for j in (m, e2):
+            for xx in range(nx):
+                for c in range(WO_CHUNKS):
+                    wo_wait(j, xx, c)
+                    go("inner", lambda j=j, xx=xx, c=c: wo_z(j, xx, c, 0, e))
+        for pair in far:
+            mix_wait(*pair, rows)
+
+        def away(c):
+            return remote(
+                out_away.at[c], out_buf.at[x, :, cols(c)], s_out.at[c], r_out.at[c], dev(f, z, other)
+            )
+
+        for c in range(WO_CHUNKS):
+            block = wo_buf[x, :, cols(c)]
+            out_away[c] = jnp.dot(
+                mix_buf[tile(other, tok), :], block, preferred_element_type=f32
+            ).astype(bf16)
+            go("inner", lambda c=c: away(c))
+            out_buf[x, :, cols(c)] = jnp.dot(
+                mix_buf[tile(x, tok), :], block, preferred_element_type=f32
+            ).astype(bf16)
+            result(x, c).start()
+        for c in range(WO_CHUNKS):
+            ref = out_buf.at[other, :, cols(c)]
+            remote(ref, ref, s_out.at[c], r_out.at[c], here).wait_recv()
+            result(other, c).start()
+
+    @pl.when(is_end)
+    def _():
+        def cross(j):
+            for xx in range(nx):
+                for c in range(WO_CHUNKS):
+                    wo_wait(j, xx, c)
+                    go("end", lambda xx=xx, c=c: wo_cross(j, xx, c))
+
+        cross(n)
+        for pair in far:
+            mix_wait(*pair, tok)
+        cross(m)
+        cross(e2)
+        for c in range(WO_CHUNKS):
+            out_buf[x, :, cols(c)] = jnp.dot(
+                mix_buf[0:tok, :], wo_buf[x, :, cols(c)], preferred_element_type=f32
+            ).astype(bf16)
+            result(x, c).start()
+        for c in range(WO_CHUNKS):
+            wox_wait(z, other, c)
+            for j in (n, m, e2):
+                for xx in range(nx):
+                    wox_wait(j, xx, c)
+        for c in range(WO_CHUNKS):
+            out_buf[other, :, cols(c)] = jnp.dot(
+                mix_buf[0:tok, :], wo_buf[other, :, cols(c)], preferred_element_type=f32
+            ).astype(bf16)
+            result(other, c).start()
+
+    for make in pending["all"]:
+        make().wait_send()
+    for kind, cond in (("end", is_end), ("inner", is_inner)):
+        @pl.when(cond)
+        def _():
+            for make in pending[kind]:
+                make().wait_send()
+
     for d in range(1, nf):
-        kvp_send(d).wait_send()
         q_send(lax.rem(f + d, nf)).wait_send()
-    for pair in pairs[1:]:
-        kv_send(1, *pair).wait_send()
-        mix_send(*pair).wait_send()
 
     @pl.when(z < nz - 1)
     def _():
@@ -606,21 +654,9 @@
         for pair in pairs[1:]:
             kv_send(0, *pair).wait_send()
 
-    for j in range(nz):
-        for c in range(WO_CHUNKS):
-            wo_cross(j, c).wait_send()
-
-        @pl.when((z < nz - 1) & (z >= j))
-        def _():
-            wq_copy(wq, j, True).wait_send()
-            for c in range(WO_CHUNKS):
-                wo_copy(j, c, True).wait_send()
-
-        @pl.when((z > 0) & (z <= j))
-        def _():
-            wq_copy(wq, j, False).wait_send()
-            for c in range(WO_CHUNKS):
-                wo_copy(j, c, False).wait_send()
+    for h in range(nx):
+        for c in range(WO_CHUNKS):
+            result(h, c).wait()
 
 
 def fused_on_device(nf, nz, nx, hidden, w_query, w_keyvalue, w_output, segment_ids):
@@ -629,14 +665,17 @@
     rows = tok * nx
     sub = rows // nf
     kvw = w_keyvalue.shape[1]
+    heads = nz * nx
+    part = cols // nx
     f32, bf16 = jnp.float32, jnp.bfloat16
     dma = pltpu.SemaphoreType.DMA
     vmem = pl.BlockSpec(memory_space=pltpu.VMEM)
+    anywhere = pl.BlockSpec(memory_space=pl.ANY)
     scratch = [
         pltpu.VMEM((rows, kdim), bf16),
         pltpu.VMEM((nz, kdim, HD), bf16),
         pltpu.VMEM((nz * kvw, kdim), bf16),
-        pltpu.VMEM((nz * nx * HD, cols), bf16),
+        pltpu.VMEM((nx, heads * HD, part), bf16),
         pltpu.VMEM((2, nx, 1, tok), jnp.int32),
         pltpu.VMEM((nz, rows, HD), f32),
         pltpu.VMEM((nf, rows, HD), f32),
@@ -645,21 +684,25 @@
         pltpu.VMEM((sub, HD), bf16),
         pltpu.VMEM((2, nx, rows, HD), bf16),
         pltpu.VMEM((rows, HD), bf16),
-        pltpu.VMEM((tok, nz * nx * HD), bf16),
+        pltpu.VMEM((rows, heads * HD), bf16),
         pltpu.VMEM((rows, HD), f32),
         pltpu.VMEM((rows, HD), f32),
+        pltpu.VMEM((nx, tok, part), bf16),
+        pltpu.VMEM((WO_CHUNKS, tok, part // WO_CHUNKS), bf16),
         dma((7,)), dma, dma, dma((1 + nx,)), dma((2, nx)),
-        dma((nz,)), dma((nz,)), dma((nz,)), dma((nz,)), dma((nz,)),
+        dma((2, nz)), dma((nz,)), dma((2, nz)), dma((nz,)),
         dma((nz,)), dma((nf,)), dma((nf,)), dma((nf,)),
         dma((2, nx, nf)), dma((2, nx, nf)),
-        dma((nz, WO_CHUNKS)), dma((nz, WO_CHUNKS)), dma((nz, WO_CHUNKS)),
-        dma((nz * nx, WO_CHUNKS)), dma((nx, nf)), dma((nx, nf)),
+        dma((2, nz, nx, WO_CHUNKS)), dma((nz, nx, WO_CHUNKS)),
+        dma((nz + 1, nx, WO_CHUNKS)), dma((nz, nx, WO_CHUNKS)),
+        dma((nx, nf)), dma((nx, nf)),
+        dma((WO_CHUNKS,)), dma((WO_CHUNKS,)), dma((nx, WO_CHUNKS)),
     ]
     return pl.pallas_call(
         functools.partial(fused_kernel, nf, nz, nx),
         out_shape=jax.ShapeDtypeStruct((tok, cols), bf16),
-        in_specs=[vmem] * 5,
-        out_specs=vmem,
+        in_specs=[anywhere] * 4 + [vmem],
+        out_specs=anywhere,
         scratch_shapes=scratch,
         name="fused_sublayer",
         compiler_params=pltpu.CompilerParams(

time: 105 us -> 114 us (1.086)
  Pallas kernels: 103 us -> 112 us
    pallas_call x1, Pallas kernels: 103 us -> 112 us  [fused_on_device(): pl.pallas_call(functools.partial(fused_kernel, nf, nz, nx), out_shape=jax...]
where the time goes in v1:
time: 114 us
  Pallas kernels  112 us (98%)
  local copies, waits for them, and re-layouts  2.3 us (2%)
    pallas_call x1, Pallas kernels, fused_on_device(): pl.pallas_call(functools.partial(fused_kernel, nf, nz, nx), out_shape=jax...  112 us
    unnamed x1, local copies, waits for them, and re-layouts  2.3 us

profile of v1, /device:TPU:24, one launch (start us, length us, event | category | flops | bytes accessed | tf_op | source)
XLA Modules:
  0.0 114.1 jit_solution(11627257403550748411)
XLA Ops:
  0.0 111.8 %fused_sublayer.1 = bf16[256,2048]{1,0:T(8,128)(2,1)} custom-call(bf16[256,2048]{1,0:T(8,128)(2,1)} %hid.1, bf16[2048,128]{1,0:T(8,128)(2,1)} %wq.1, bf16[32,2048]{1,0:T(8,128)(2,1)} %bitcast.2, bf16[128,2048]{1,0:T(8,128)(2,1)} %wo.1, s32[1,256]{1,0:T(1,128)} %bitcast.3), custom_call_target="tpu_custom_call" | custom-call | tf_op jit(solution)/shard_map/fused_sublayer/pallas_call | solution.py:701
  111.8 2.3 %copy.7 = bf16[256,2048]{1,0:T(8,128)(2,1)} copy(bf16[256,2048]{1,0:T(8,128)(2,1)} %fused_sublayer.1) | data formatting | bytes 2097152

commit v2 on v1

--- a/solution.py
+++ b/solution.py
@@ -131,16 +131,18 @@
 
 NEG_POS = -1
 WO_CHUNKS = 4
+MOVED = 4
+END_CHUNKS = 2
 
 
 def fused_kernel(
     nf, nz, nx, hid, wq, wkv, wo, seg, out,
     h_buf, wq_buf, wkv_buf, wo_buf, seg_buf,
     q_part, q_recv, kv_part, kv_recv, kv_piece, kv_all, mix_own, mix_buf, q_cos, q_sin,
-    out_buf, out_away,
+    out_buf, out_away, h_end, e_part, e_recv, e_back, q_in,
     s_loc, s_hid, r_hid, s_seg, r_seg, s_wkv, r_wkv, s_wq, r_wq,
     s_q, r_q, s_kvp, r_kvp, s_kv, r_kv, s_wo, r_wo, s_wox, r_wox, s_mix, r_mix,
-    s_out, r_out, s_res,
+    s_out, r_out, s_res, s_he, r_he, s_hx, s_ep, r_ep, s_eb, r_eb,
 ):
     f = lax.axis_index("fsdp")
     s = lax.axis_index("sp")
@@ -150,6 +152,8 @@
     sub = rows // nf
     kvw = wkv.shape[0]
     other = 1 - x
+    moved = kdim * MOVED // 8
+    block = tok // 2
     half_cols = wo.shape[1] // nx
     chunk = half_cols // WO_CHUNKS
     f32, bf16 = jnp.float32, jnp.bfloat16
@@ -215,11 +219,25 @@
         wkv_z(j, 0, z).wait_recv()
 
     def wq_z(j, d, target):
-        ref = wq_buf.at[j]
+        ref = wq_buf.at[j] if d else wq_buf.at[j, moved:, :]
         return remote(ref, ref, s_wq.at[d, j], r_wq.at[j], dev(f, target, x))
 
-    def wq_wait(j):
-        wq_z(j, 0, z).wait_recv()
+    def wq_wait(j, d=1):
+        wq_z(j, d, z).wait_recv()
+
+    def he_z(hf):
+        rows_of = pl.ds(pl.multiple_of(x * tok + hf * block, block), block)
+        return remote(
+            h_buf.at[rows_of, 0:moved], h_end.at[x, hf], s_he.at[hf], r_he.at[x, hf], dev(f, n, x)
+        )
+
+    def he_x(hf):
+        ref = h_end.at[x, hf]
+        return remote(ref, ref, s_hx.at[hf], r_he.at[x, hf], dev(f, z, other))
+
+    def he_wait(xx, hf):
+        ref = h_end.at[xx, hf]
+        remote(ref, ref, s_hx.at[hf], r_he.at[xx, hf], here).wait_recv()
 
     def wo_unit(h, j, xx, c):
         return wo_buf.at[h, tile(j * nx + xx, HD), cols(c)]
@@ -296,20 +314,29 @@
 
     for copy in own_wo:
         copy.wait()
-    for c in range(WO_CHUNKS):
-        go("all", lambda c=c: wo_pair(c))
 
     @pl.when(is_end)
     def _():
-        for c in range(WO_CHUNKS):
-            go("end", lambda c=c: wo_z(z, x, c, 1, n))
-        for c in range(WO_CHUNKS):
+        for hf in range(2):
+            go("end", lambda hf=hf: he_z(hf))
+        for c in range(WO_CHUNKS):
+            go("end", lambda c=c: wo_pair(c))
+        for c in range(END_CHUNKS):
             go("end", lambda c=c: wo_cross(z, x, c))
+
+    @pl.when(is_inner)
+    def _():
+        for c in range(WO_CHUNKS):
+            go("inner", lambda c=c: wo_z(z, x, c, 0, e))
 
     @pl.when(z == 0)
     def _():
         kv_all[0] = jnp.zeros(kv_all.shape[1:], bf16)
         seg_buf[0] = jnp.full(seg_buf.shape[1:], NEG_POS, jnp.int32)
+
+    @pl.when(is_inner)
+    def _():
+        q_in[...] = jnp.zeros(q_in.shape, f32)
 
     def table(row_count, first, lane_index):
         position = (first + lax.broadcasted_iota(jnp.int32, (row_count, HD), 0)).astype(f32)
@@ -332,12 +359,53 @@
     def q_send(j):
         return remote(q_part.at[j], q_recv.at[f], s_q.at[j], r_q.at[f], (j, s))
 
-    def q_project(j):
-        q_part[j] = jnp.dot(h_buf[...], wq_buf[j], preferred_element_type=f32)
-
+    def q_spread(j):
         @pl.when(j != f)
         def _():
             q_send(j).start()
+
+    def q_project(j):
+        q_part[j] = jnp.dot(h_buf[...], wq_buf[j], preferred_element_type=f32)
+        q_spread(j)
+
+    def q_kept(j):
+        q_part[j] = jnp.dot(
+            h_buf[:, moved:], wq_buf[j, moved:, :], preferred_element_type=f32
+        )
+        q_spread(j)
+
+    def e_send(j, xx, hf):
+        return remote(
+            e_part.at[j, xx, hf], e_recv.at[f, xx, hf], s_ep.at[j, xx, hf], r_ep.at[f, xx, hf], (j, s)
+        )
+
+    def e_project(xx, hf, blocks):
+        for j in blocks:
+            e_part[j, xx, hf] = jnp.dot(
+                h_end[xx, hf], wq_buf[j, 0:moved, :], preferred_element_type=f32
+            )
+
+            @pl.when(j != f)
+            def _():
+                e_send(j, xx, hf).start()
+
+
+    def e_return(xx, hf):
+        return remote(
+            e_back.at[xx, hf], q_in.at[xx, hf], s_eb.at[xx, hf], r_eb.at[xx, hf], dev(f, e, x)
+        )
+
+    def e_collect(xx, hf):
+        part = e_part[f, xx, hf]
+        for d in range(1, nf):
+            ff = lax.rem(f + d, nf)
+            remote(
+                e_recv.at[ff, xx, hf], e_recv.at[ff, xx, hf],
+                s_ep.at[0, xx, hf], r_ep.at[ff, xx, hf], here,
+            ).wait_recv()
+            part = part + e_recv[ff, xx, hf]
+        e_back[xx, hf] = part
+        go("inner", lambda: e_return(xx, hf))
 
     @pl.when(is_inner)
     def _():
@@ -347,32 +415,25 @@
         go("inner", lambda: wkv_z(m, 0, e))
         wq_wait(e)
         go("inner", lambda: wq_z(e, 1, m))
-        for c in range(WO_CHUNKS):
-            go("inner", lambda c=c: wo_z(z, x, c, 1, m))
         wq_wait(m)
         go("inner", lambda: wq_z(m, 0, e))
         wkv_wait(e2)
         go("inner", lambda: wkv_z(e2, 0, e))
+        he_wait(x, 0)
+        go("inner", lambda: he_x(0))
 
     hid_wait()
-    q_project(z)
-
-    @pl.when(is_inner)
-    def _():
-        q_project(e)
-        q_project(m)
-        wq_wait(e2)
-        go("inner", lambda: wq_z(e2, 0, e))
+
+    @pl.when(is_inner)
+    def _():
+        for j in (z, e, m):
+            q_project(j)
 
     @pl.when(is_end)
     def _():
-        wq_wait(n)
-        q_project(n)
-        for c in range(WO_CHUNKS):
-            wo_wait(z, other, c)
-            go("end", lambda c=c: wo_z(z, other, c, 1, n))
-        wq_wait(m)
-        q_project(m)
+        q_kept(z)
+        wq_wait(n, 0)
+        q_kept(n)
         for j in (n, m, e2):
             wkv_wait(j)
 
@@ -397,14 +458,16 @@
 
     @pl.when(is_inner)
     def _():
-        q_project(e2)
-        for c in range(WO_CHUNKS):
-            go("inner", lambda c=c: wo_z(z, x, c, 0, e))
-        for c in range(WO_CHUNKS):
-            wo_wait(z, other, c)
-            go("inner", lambda c=c: wo_z(z, other, c, 1, m))
-        for c in range(WO_CHUNKS):
-            go("inner", lambda c=c: wo_z(z, other, c, 0, e))
+        he_wait(x, 1)
+        go("inner", lambda: he_x(1))
+        for c in range(WO_CHUNKS):
+            go("inner", lambda c=c: wo_pair(c))
+        e_project(x, 0, (z, e, m))
+
+    @pl.when(is_end)
+    def _():
+        wq_wait(m, 0)
+        q_kept(m)
 
     total = kv_part[tile(f, sub), :]
     for d in range(1, nf):
@@ -447,12 +510,26 @@
     def _():
         kv_next().start()
 
-    @pl.when(is_inner)
-    def _():
-        for xx in range(nx):
-            for c in range(WO_CHUNKS):
-                wo_wait(e, xx, c)
-                go("inner", lambda xx=xx, c=c: wo_z(e, xx, c, 1, m))
+    @pl.when(is_end)
+    def _():
+        for c in range(WO_CHUNKS):
+            go("end", lambda c=c: wo_z(z, x, c, 1, n))
+        for c in range(WO_CHUNKS):
+            wo_wait(z, other, c)
+            go("end", lambda c=c: wo_z(z, other, c, 1, n))
+
+    @pl.when(is_inner)
+    def _():
+        for c in range(WO_CHUNKS):
+            go("inner", lambda c=c: wo_z(z, x, c, 1, m))
+        wq_wait(e2)
+        go("inner", lambda: wq_z(e2, 0, e))
+        q_project(e2)
+        e_project(x, 0, (e2,))
+        he_wait(other, 0)
+        e_project(other, 0, (z, e, m, e2))
+        e_project(x, 1, (z, e, m, e2))
+        e_collect(x, 0)
 
     @pl.when(z > 0)
     def _():
@@ -460,16 +537,33 @@
         for pair in pairs[1:]:
             kv_send(0, *pair).start()
 
+    @pl.when(is_inner)
+    def _():
+        he_wait(other, 1)
+        e_project(other, 1, (z, e, m, e2))
+        for c in range(WO_CHUNKS):
+            wo_wait(m, x, c)
+            go("inner", lambda c=c: wo_z(m, x, c, 0, e))
+        e_collect(other, 0)
+        e_collect(x, 1)
+
     @pl.when(is_end)
     def _():
-        wq_wait(e2)
-        q_project(e2)
+        wq_wait(e2, 0)
+        q_kept(e2)
+        for xx in range(nx):
+            for hf in range(2):
+                remote(
+                    q_in.at[xx, hf], q_in.at[xx, hf], s_eb.at[xx, hf], r_eb.at[xx, hf], here
+                ).wait_recv()
 
     q_total = q_part[f]
     for d in range(1, nf):
         ff = lax.rem(f + d, nf)
         remote(q_part.at[0], q_recv.at[ff], s_q.at[0], r_q.at[ff], here).wait_recv()
         q_total = q_total + q_recv[ff]
+    returned = q_in[...].reshape(rows, HD)
+    q_total = q_total + jnp.where(is_end, returned, 0.0)
     q_turned = q_total * q_cos[...] + pltpu.roll(q_total, half, 1) * q_sin[...]
     q_head = q_turned.astype(bf16).astype(f32)
     quarters = []
@@ -534,40 +628,59 @@
 
     head = f * nx + x
 
-    def mix_part(dx, d):
-        ff, xx = lax.rem(f + d, nf), lax.rem(x + dx, nx)
-        return remote(
-            mix_own.at[tile(xx, tok)], mix_buf.at[0:tok, tile(head, HD)],
-            s_mix.at[dx, d], r_mix.at[x, f], dev(ff, z, xx),
-        )
-
-    def mix_whole(dx, d):
-        ff, xx = lax.rem(f + d, nf), lax.rem(x + dx, nx)
-        return remote(
-            mix_own, mix_buf.at[:, tile(head, HD)],
-            s_mix.at[dx, d], r_mix.at[x, f], dev(ff, z, xx),
-        )
-
-    def mix_wait(dx, d, count):
-        ff, xx = lax.rem(f + d, nf), lax.rem(x + dx, nx)
-        ref = mix_buf.at[0:count, tile(ff * nx + xx, HD)]
+    ahead = lax.rem(f + 2, nf)
+    beside = f + 1 - 2 * lax.rem(f, 2)
+    across = lax.rem(beside + 2, nf)
+
+    def mix_of(ff, xx):
+        return mix_buf.at[:, tile(ff * nx + xx, HD)]
+
+    def mix_send(ff, xx, hop):
+        target = (dev(f, z, other), dev(ahead, z, x), dev(beside, z, x))[hop]
+        return remote(
+            mix_of(ff, xx), mix_of(ff, xx), s_mix.at[hop, xx, ff], r_mix.at[xx, ff], target
+        )
+
+    def mix_wait(ff, xx):
         remote(
-            ref, ref, s_mix.at[dx, d], r_mix.at[xx, ff], here,
+            mix_of(ff, xx), mix_of(ff, xx), s_mix.at[0, xx, ff], r_mix.at[xx, ff], here
         ).wait_recv()
 
-    far = [pair for pair in pairs[1:] if pair[0]] + [pair for pair in pairs[1:] if not pair[0]]
+    mix_buf[:, tile(head, HD)] = mix_own[...]
+    for hop in range(3):
+        go("all", lambda hop=hop: mix_send(f, x, hop))
+
+    @pl.when(is_inner)
+    def _():
+        e_collect(other, 1)
+        for c in range(WO_CHUNKS):
+            wo_wait(z, other, c)
+            go("inner", lambda c=c: wo_z(z, other, c, 1, m))
+            go("inner", lambda c=c: wo_z(z, other, c, 0, e))
 
     @pl.when(is_end)
     def _():
-        for pair in far:
-            go("end", lambda pair=pair: mix_part(*pair))
-        mix_buf[0:tok, tile(head, HD)] = mix_own[tile(x, tok), :]
-
-    @pl.when(is_inner)
-    def _():
-        for pair in far:
-            go("inner", lambda pair=pair: mix_whole(*pair))
-        mix_buf[:, tile(head, HD)] = mix_own[...]
+        for xx in (x, other):
+            for c in range(WO_CHUNKS):
+                wo_wait(n, xx, c)
+                if c < END_CHUNKS:
+                    go("end", lambda xx=xx, c=c: wo_cross(n, xx, c))
+
+    mix_wait(f, other)
+    for hop in (1, 2):
+        go("all", lambda hop=hop: mix_send(f, other, hop))
+    mix_wait(ahead, x)
+    go("all", lambda: mix_send(ahead, x, 2))
+
+    @pl.when(is_inner)
+    def _():
+        for xx in (x, other):
+            for c in range(WO_CHUNKS):
+                wo_wait(e, xx, c)
+                go("inner", lambda xx=xx, c=c: wo_z(e, xx, c, 1, m))
+
+    mix_wait(ahead, other)
+    go("all", lambda: mix_send(ahead, other, 2))
 
     def result(h, c):
         where = pl.ds(pl.multiple_of(h * half_cols + c * chunk, chunk), chunk)
@@ -575,62 +688,77 @@
 
     @pl.when(is_inner)
     def _():
+        for c in range(WO_CHUNKS):
+            wo_wait(m, other, c)
+            go("inner", lambda c=c: wo_z(m, other, c, 0, e))
+        for xx in (x, other):
+            for c in range(WO_CHUNKS):
+                wo_wait(e2, xx, c)
+                go("inner", lambda xx=xx, c=c: wo_z(e2, xx, c, 0, e))
+
+    for ff in (beside, across):
+        for xx in (x, other):
+            mix_wait(ff, xx)
+
+    @pl.when(is_end)
+    def _():
         for j in (m, e2):
-            for xx in range(nx):
+            for xx in (x, other):
                 for c in range(WO_CHUNKS):
                     wo_wait(j, xx, c)
-                    go("inner", lambda j=j, xx=xx, c=c: wo_z(j, xx, c, 0, e))
-        for pair in far:
-            mix_wait(*pair, rows)
-
-        def away(c):
-            return remote(
-                out_away.at[c], out_buf.at[x, :, cols(c)], s_out.at[c], r_out.at[c], dev(f, z, other)
-            )
-
-        for c in range(WO_CHUNKS):
-            block = wo_buf[x, :, cols(c)]
-            out_away[c] = jnp.dot(
-                mix_buf[tile(other, tok), :], block, preferred_element_type=f32
-            ).astype(bf16)
-            go("inner", lambda c=c: away(c))
-            out_buf[x, :, cols(c)] = jnp.dot(
-                mix_buf[tile(x, tok), :], block, preferred_element_type=f32
-            ).astype(bf16)
-            result(x, c).start()
-        for c in range(WO_CHUNKS):
-            ref = out_buf.at[other, :, cols(c)]
-            remote(ref, ref, s_out.at[c], r_out.at[c], here).wait_recv()
-            result(other, c).start()
+                    if c < END_CHUNKS:
+                        go("end", lambda j=j, xx=xx, c=c: wo_cross(j, xx, c))
+
+    def product(h, c, row_tile):
+        return jnp.dot(
+            mix_buf[tile(row_tile, tok), :], wo_buf[h, :, cols(c)], preferred_element_type=f32
+        ).astype(bf16)
+
+    def away(c):
+        return remote(
+            out_away.at[c], out_buf.at[x, :, cols(c)], s_out.at[c], r_out.at[c], dev(f, z, other)
+        )
+
+    def away_stage(kind, c):
+        out_away[c] = product(x, c, other)
+        go(kind, lambda: away(c))
+
+    def own_stage(h, c):
+        out_buf[h, :, cols(c)] = product(h, c, x)
+        result(h, c).start()
+
+    def away_wait(c):
+        ref = out_buf.at[other, :, cols(c)]
+        remote(ref, ref, s_out.at[c], r_out.at[c], here).wait_recv()
+        result(other, c).start()
+
+    for c in range(END_CHUNKS, WO_CHUNKS):
+        away_stage("all", c)
+
+    @pl.when(is_inner)
+    def _():
+        for c in range(END_CHUNKS):
+            away_stage("inner", c)
+
+    for c in range(WO_CHUNKS):
+        own_stage(x, c)
 
     @pl.when(is_end)
     def _():
-        def cross(j):
-            for xx in range(nx):
-                for c in range(WO_CHUNKS):
-                    wo_wait(j, xx, c)
-                    go("end", lambda xx=xx, c=c: wo_cross(j, xx, c))
-
-        cross(n)
-        for pair in far:
-            mix_wait(*pair, tok)
-        cross(m)
-        cross(e2)
-        for c in range(WO_CHUNKS):
-            out_buf[x, :, cols(c)] = jnp.dot(
-                mix_buf[0:tok, :], wo_buf[x, :, cols(c)], preferred_element_type=f32
-            ).astype(bf16)
-            result(x, c).start()
-        for c in range(WO_CHUNKS):
+        for c in range(END_CHUNKS):
             wox_wait(z, other, c)
             for j in (n, m, e2):
                 for xx in range(nx):
                     wox_wait(j, xx, c)
-        for c in range(WO_CHUNKS):
-            out_buf[other, :, cols(c)] = jnp.dot(
-                mix_buf[0:tok, :], wo_buf[other, :, cols(c)], preferred_element_type=f32
-            ).astype(bf16)
-            result(other, c).start()
+            own_stage(other, c)
+
+    for c in range(END_CHUNKS, WO_CHUNKS):
+        away_wait(c)
+
+    @pl.when(is_inner)
+    def _():
+        for c in range(END_CHUNKS):
+            away_wait(c)
 
     for make in pending["all"]:
         make().wait_send()
@@ -642,6 +770,13 @@
 
     for d in range(1, nf):
         q_send(lax.rem(f + d, nf)).wait_send()
+
+    @pl.when(is_inner)
+    def _():
+        for d in range(1, nf):
+            for xx in range(nx):
+                for hf in range(2):
+                    e_send(lax.rem(f + d, nf), xx, hf).wait_send()
 
     @pl.when(z < nz - 1)
     def _():
@@ -689,14 +824,21 @@
         pltpu.VMEM((rows, HD), f32),
         pltpu.VMEM((nx, tok, part), bf16),
         pltpu.VMEM((WO_CHUNKS, tok, part // WO_CHUNKS), bf16),
+        pltpu.VMEM((nx, 2, tok // 2, kdim * MOVED // 8), bf16),
+        pltpu.VMEM((nz, nx, 2, tok // 2, HD), f32),
+        pltpu.VMEM((nf, nx, 2, tok // 2, HD), f32),
+        pltpu.VMEM((nx, 2, tok // 2, HD), f32),
+        pltpu.VMEM((nx, 2, tok // 2, HD), f32),
         dma((7,)), dma, dma, dma((1 + nx,)), dma((2, nx)),
         dma((2, nz)), dma((nz,)), dma((2, nz)), dma((nz,)),
         dma((nz,)), dma((nf,)), dma((nf,)), dma((nf,)),
         dma((2, nx, nf)), dma((2, nx, nf)),
         dma((2, nz, nx, WO_CHUNKS)), dma((nz, nx, WO_CHUNKS)),
         dma((nz + 1, nx, WO_CHUNKS)), dma((nz, nx, WO_CHUNKS)),
-        dma((nx, nf)), dma((nx, nf)),
+        dma((3, nx, nf)), dma((nx, nf)),
         dma((WO_CHUNKS,)), dma((WO_CHUNKS,)), dma((nx, WO_CHUNKS)),
+        dma((2,)), dma((nx, 2)), dma((2,)), dma((nz, nx, 2)), dma((nf, nx, 2)),
+        dma((nx, 2)), dma((nx, 2)),
     ]
     return pl.pallas_call(
         functools.partial(fused_kernel, nf, nz, nx),

time: 114 us -> 113 us (level)
  the two profiles are of different devices: /device:TPU:24 before, /device:TPU:0 now
where the time goes in v2:
time: 113 us
  Pallas kernels  111 us (98%)
  local copies, waits for them, and re-layouts  2.3 us (2%)
    pallas_call x1, Pallas kernels, fused_on_device(): pl.pallas_call(functools.partial(fused_kernel, nf, nz, nx), out_shape=jax...  111 us
    unnamed x1, local copies, waits for them, and re-layouts  2.3 us

profile of v2, /device:TPU:0, one launch (start us, length us, event | category | flops | bytes accessed | tf_op | source)
XLA Modules:
  0.0 113.3 jit_solution(10002885156659645214)
XLA Ops:
  0.0 111.0 %fused_sublayer.1 = bf16[256,2048]{1,0:T(8,128)(2,1)} custom-call(bf16[256,2048]{1,0:T(8,128)(2,1)} %hid.1, bf16[2048,128]{1,0:T(8,128)(2,1)} %wq.1, bf16[32,2048]{1,0:T(8,128)(2,1)} %bitcast.2, bf16[128,2048]{1,0:T(8,128)(2,1)} %wo.1, s32[1,256]{1,0:T(1,128)} %bitcast.3), custom_call_target="tpu_custom_call" | custom-call | tf_op jit(solution)/shard_map/fused_sublayer/pallas_call | solution.py:843
  111.0 2.3 %copy.7 = bf16[256,2048]{1,0:T(8,128)(2,1)} copy(bf16[256,2048]{1,0:T(8,128)(2,1)} %fused_sublayer.1) | data formatting | bytes 2097152

commit v3 on v2

--- a/solution.py
+++ b/solution.py
@@ -138,11 +138,11 @@
 def fused_kernel(
     nf, nz, nx, hid, wq, wkv, wo, seg, out,
     h_buf, wq_buf, wkv_buf, wo_buf, seg_buf,
-    q_part, q_recv, kv_part, kv_recv, kv_piece, kv_all, mix_own, mix_buf, q_cos, q_sin,
-    out_buf, out_away, h_end, e_part, e_recv, e_back, q_in,
+    q_part, q_mate, q_sum, q_far, kv_part, kv_recv, kv_piece, kv_all, mix_own, mix_buf, q_cos, q_sin,
+    out_buf, out_away, h_end, e_part, e_mate, e_sum, e_far, e_back, q_in,
     s_loc, s_hid, r_hid, s_seg, r_seg, s_wkv, r_wkv, s_wq, r_wq,
-    s_q, r_q, s_kvp, r_kvp, s_kv, r_kv, s_wo, r_wo, s_wox, r_wox, s_mix, r_mix,
-    s_out, r_out, s_res, s_he, r_he, s_hx, s_ep, r_ep, s_eb, r_eb,
+    s_q, r_q, s_qf, r_qf, s_kvp, r_kvp, s_kv, r_kv, s_wo, r_wo, s_wox, r_wox, s_mix, r_mix,
+    s_out, r_out, s_res, s_he, r_he, s_hx, s_ep, r_ep, s_ef, r_ef, s_eb, r_eb,
 ):
     f = lax.axis_index("fsdp")
     s = lax.axis_index("sp")
@@ -164,6 +164,16 @@
     n = jnp.where(low, 1, nz - 2)
     m = nz - 1 - n
     e2 = nz - 1 - e
+    beside = f + 1 - 2 * lax.rem(f, 2)
+    ahead = lax.rem(f + 2, nf)
+    across = lax.rem(beside + 2, nf)
+
+    def block_of(ff):
+        return lax.rem(ff, 2) * 2 + ff // 2
+
+    core = lax.rem(f, 2)
+    mine, theirs = block_of(f), block_of(ahead)
+    near = core == z // 2
 
     def dev(ff, zz, xx):
         return (ff, zz * nx + xx)
@@ -188,7 +198,9 @@
         return slice(c * chunk, (c + 1) * chunk)
 
     own_h = pltpu.make_async_copy(hid, h_buf.at[tile(x, tok)], s_loc.at[0])
-    own_wq = pltpu.make_async_copy(wq, wq_buf.at[z], s_loc.at[1])
+    own_wq = pltpu.make_async_copy(
+        wq, wq_buf.at[z // 2, :, tile(lax.rem(z, 2), HD)], s_loc.at[1]
+    )
     own_wkv = pltpu.make_async_copy(wkv, wkv_buf.at[tile(z, kvw)], s_loc.at[2])
     own_wo = [
         pltpu.make_async_copy(
@@ -218,8 +230,11 @@
     def wkv_wait(j):
         wkv_z(j, 0, z).wait_recv()
 
+    def wq_of(j, first):
+        return wq_buf.at[j // 2, first:, tile(lax.rem(j, 2), HD)]
+
     def wq_z(j, d, target):
-        ref = wq_buf.at[j] if d else wq_buf.at[j, moved:, :]
+        ref = wq_of(j, 0) if d else wq_of(j, moved)
         return remote(ref, ref, s_wq.at[d, j], r_wq.at[j], dev(f, target, x))
 
     def wq_wait(j, d=1):
@@ -319,6 +334,8 @@
     def _():
         for hf in range(2):
             go("end", lambda hf=hf: he_z(hf))
+        for c in range(WO_CHUNKS):
+            go("end", lambda c=c: wo_z(z, x, c, 1, n))
         for c in range(WO_CHUNKS):
             go("end", lambda c=c: wo_pair(c))
         for c in range(END_CHUNKS):
@@ -356,39 +373,71 @@
     q_cos[...] = jnp.cos(q_angle)
     q_sin[...] = jnp.where(lane < half, -q_sine, q_sine)
 
+    same_core = lambda j: j // 2 == core
+
     def q_send(j):
-        return remote(q_part.at[j], q_recv.at[f], s_q.at[j], r_q.at[f], (j, s))
-
-    def q_spread(j):
-        @pl.when(j != f)
+        return remote(
+            q_part.at[j], q_mate.at[lax.rem(j, 2)], s_q.at[lax.rem(j, 2)], r_q.at[lax.rem(j, 2)], dev(beside, z, x)
+        )
+
+    def q_mate_wait(j):
+        remote(
+            q_mate.at[lax.rem(j, 2)], q_mate.at[lax.rem(j, 2)], s_q.at[0], r_q.at[lax.rem(j, 2)], here
+        ).wait_recv()
+
+    def q_far_copy():
+        return remote(q_sum, q_far, s_qf, r_qf, dev(ahead, z, x))
+
+    def q_project(j, first):
+        both = jnp.dot(
+            h_buf[:, first:], wq_buf[j // 2, first:, :], preferred_element_type=f32
+        )
+        for b in range(2):
+            q_part[j // 2 * 2 + b] = both[:, b * HD : (b + 1) * HD]
+
+        @pl.when(jnp.logical_not(same_core(j)))
         def _():
-            q_send(j).start()
-
-    def q_project(j):
-        q_part[j] = jnp.dot(h_buf[...], wq_buf[j], preferred_element_type=f32)
-        q_spread(j)
-
-    def q_kept(j):
-        q_part[j] = jnp.dot(
-            h_buf[:, moved:], wq_buf[j, moved:, :], preferred_element_type=f32
-        )
-        q_spread(j)
+            for b in range(2):
+                q_send(j // 2 * 2 + b).start()
+
+    def q_relay(far):
+        @pl.when(jnp.logical_not(near) if far else near)
+        def _():
+            q_mate_wait(theirs)
+            q_sum[...] = q_part[theirs] + q_mate[lax.rem(theirs, 2)]
+            q_far_copy().start()
 
     def e_send(j, xx, hf):
         return remote(
-            e_part.at[j, xx, hf], e_recv.at[f, xx, hf], s_ep.at[j, xx, hf], r_ep.at[f, xx, hf], (j, s)
-        )
-
-    def e_project(xx, hf, blocks):
-        for j in blocks:
-            e_part[j, xx, hf] = jnp.dot(
-                h_end[xx, hf], wq_buf[j, 0:moved, :], preferred_element_type=f32
-            )
-
-            @pl.when(j != f)
-            def _():
-                e_send(j, xx, hf).start()
-
+            e_part.at[j, xx, hf], e_mate.at[lax.rem(j, 2), xx, hf],
+            s_ep.at[lax.rem(j, 2), xx, hf], r_ep.at[lax.rem(j, 2), xx, hf], dev(beside, z, x)
+        )
+
+    def e_mate_wait(j, xx, hf):
+        ref = e_mate.at[lax.rem(j, 2), xx, hf]
+        remote(ref, ref, s_ep.at[0, xx, hf], r_ep.at[lax.rem(j, 2), xx, hf], here).wait_recv()
+
+    def e_far_copy(xx, hf):
+        return remote(
+            e_sum.at[xx, hf], e_far.at[xx, hf], s_ef.at[xx, hf], r_ef.at[xx, hf], dev(ahead, z, x)
+        )
+
+    def e_project(xx, hf, j):
+        both = jnp.dot(
+            h_end[xx, hf], wq_buf[j // 2, 0:moved, :], preferred_element_type=f32
+        )
+        for b in range(2):
+            e_part[j // 2 * 2 + b, xx, hf] = both[:, b * HD : (b + 1) * HD]
+
+        @pl.when(jnp.logical_not(same_core(j)))
+        def _():
+            for b in range(2):
+                e_send(j // 2 * 2 + b, xx, hf).start()
+
+    def e_relay(xx, hf):
+        e_mate_wait(theirs, xx, hf)
+        e_sum[xx, hf] = e_part[theirs, xx, hf] + e_mate[lax.rem(theirs, 2), xx, hf]
+        e_far_copy(xx, hf).start()
 
     def e_return(xx, hf):
         return remote(
@@ -396,15 +445,12 @@
         )
 
     def e_collect(xx, hf):
-        part = e_part[f, xx, hf]
-        for d in range(1, nf):
-            ff = lax.rem(f + d, nf)
-            remote(
-                e_recv.at[ff, xx, hf], e_recv.at[ff, xx, hf],
-                s_ep.at[0, xx, hf], r_ep.at[ff, xx, hf], here,
-            ).wait_recv()
-            part = part + e_recv[ff, xx, hf]
-        e_back[xx, hf] = part
+        e_mate_wait(mine, xx, hf)
+        ref = e_far.at[xx, hf]
+        remote(ref, ref, s_ef.at[xx, hf], r_ef.at[xx, hf], here).wait_recv()
+        e_back[xx, hf] = (
+            e_part[mine, xx, hf] + e_mate[lax.rem(mine, 2), xx, hf] + e_far[xx, hf]
+        )
         go("inner", lambda: e_return(xx, hf))
 
     @pl.when(is_inner)
@@ -415,6 +461,8 @@
         go("inner", lambda: wkv_z(m, 0, e))
         wq_wait(e)
         go("inner", lambda: wq_z(e, 1, m))
+        for c in range(WO_CHUNKS):
+            go("inner", lambda c=c: wo_z(z, x, c, 1, m))
         wq_wait(m)
         go("inner", lambda: wq_z(m, 0, e))
         wkv_wait(e2)
@@ -424,16 +472,8 @@
 
     hid_wait()
 
-    @pl.when(is_inner)
-    def _():
-        for j in (z, e, m):
-            q_project(j)
-
     @pl.when(is_end)
     def _():
-        q_kept(z)
-        wq_wait(n, 0)
-        q_kept(n)
         for j in (n, m, e2):
             wkv_wait(j)
 
@@ -458,16 +498,22 @@
 
     @pl.when(is_inner)
     def _():
+        q_project(z, 0)
         he_wait(x, 1)
         go("inner", lambda: he_x(1))
-        for c in range(WO_CHUNKS):
-            go("inner", lambda c=c: wo_pair(c))
-        e_project(x, 0, (z, e, m))
+        q_relay(False)
+        e_project(x, 0, z)
+
+        @pl.when(near)
+        def _():
+            e_relay(x, 0)
+
 
     @pl.when(is_end)
     def _():
-        wq_wait(m, 0)
-        q_kept(m)
+        wq_wait(n, 0)
+        q_project(z, moved)
+        q_relay(False)
 
     total = kv_part[tile(f, sub), :]
     for d in range(1, nf):
@@ -513,23 +559,28 @@
     @pl.when(is_end)
     def _():
         for c in range(WO_CHUNKS):
-            go("end", lambda c=c: wo_z(z, x, c, 1, n))
-        for c in range(WO_CHUNKS):
             wo_wait(z, other, c)
             go("end", lambda c=c: wo_z(z, other, c, 1, n))
 
     @pl.when(is_inner)
     def _():
-        for c in range(WO_CHUNKS):
-            go("inner", lambda c=c: wo_z(z, x, c, 1, m))
         wq_wait(e2)
         go("inner", lambda: wq_z(e2, 0, e))
-        q_project(e2)
-        e_project(x, 0, (e2,))
+        q_project(e2, 0)
+        e_project(x, 0, e2)
+        e_project(x, 1, z)
+        e_project(x, 1, e2)
+
+        @pl.when(jnp.logical_not(near))
+        def _():
+            e_relay(x, 0)
+
+        e_relay(x, 1)
+        q_relay(True)
         he_wait(other, 0)
-        e_project(other, 0, (z, e, m, e2))
-        e_project(x, 1, (z, e, m, e2))
-        e_collect(x, 0)
+        e_project(other, 0, z)
+        e_project(other, 0, e2)
+        e_relay(other, 0)
 
     @pl.when(z > 0)
     def _():
@@ -539,29 +590,49 @@
 
     @pl.when(is_inner)
     def _():
+        for c in range(WO_CHUNKS):
+            go("inner", lambda c=c: wo_pair(c))
+        for c in range(WO_CHUNKS):
+            wo_wait(e, x, c)
+            go("inner", lambda c=c: wo_z(e, x, c, 1, m))
+        e_collect(x, 0)
         he_wait(other, 1)
-        e_project(other, 1, (z, e, m, e2))
+        e_project(other, 1, z)
+        e_project(other, 1, e2)
         for c in range(WO_CHUNKS):
             wo_wait(m, x, c)
             go("inner", lambda c=c: wo_z(m, x, c, 0, e))
         e_collect(other, 0)
+        e_relay(other, 1)
         e_collect(x, 1)
+        for c in range(WO_CHUNKS):
+            wo_wait(e, other, c)
+            go("inner", lambda c=c: wo_z(e, other, c, 1, m))
+        e_collect(other, 1)
+
+    def cross(j, xx):
+        for c in range(WO_CHUNKS):
+            wo_wait(j, xx, c)
+            if c < END_CHUNKS:
+                go("end", lambda c=c: wo_cross(j, xx, c))
 
     @pl.when(is_end)
     def _():
+        cross(n, x)
+        wq_wait(m, 0)
         wq_wait(e2, 0)
-        q_kept(e2)
+        q_project(e2, moved)
+        q_relay(True)
+        cross(m, x)
         for xx in range(nx):
             for hf in range(2):
                 remote(
                     q_in.at[xx, hf], q_in.at[xx, hf], s_eb.at[xx, hf], r_eb.at[xx, hf], here
                 ).wait_recv()
 
-    q_total = q_part[f]
-    for d in range(1, nf):
-        ff = lax.rem(f + d, nf)
-        remote(q_part.at[0], q_recv.at[ff], s_q.at[0], r_q.at[ff], here).wait_recv()
-        q_total = q_total + q_recv[ff]
+    q_mate_wait(mine)
+    remote(q_far, q_far, s_qf, r_qf, here).wait_recv()
+    q_total = q_part[mine] + q_mate[lax.rem(mine, 2)] + q_far[...]
     returned = q_in[...].reshape(rows, HD)
     q_total = q_total + jnp.where(is_end, returned, 0.0)
     q_turned = q_total * q_cos[...] + pltpu.roll(q_total, half, 1) * q_sin[...]
@@ -626,14 +697,10 @@
             mixed = value if mixed is None else jnp.where(lane_block % nx == xx, value, mixed)
         mix_own[span, :] = (mixed / row_total).astype(bf16)
 
-    head = f * nx + x
-
-    ahead = lax.rem(f + 2, nf)
-    beside = f + 1 - 2 * lax.rem(f, 2)
-    across = lax.rem(beside + 2, nf)
+    head = mine * nx + x
 
     def mix_of(ff, xx):
-        return mix_buf.at[:, tile(ff * nx + xx, HD)]
+        return mix_buf.at[:, tile(block_of(ff) * nx + xx, HD)]
 
     def mix_send(ff, xx, hop):
         target = (dev(f, z, other), dev(ahead, z, x), dev(beside, z, x))[hop]
@@ -652,19 +719,17 @@
 
     @pl.when(is_inner)
     def _():
-        e_collect(other, 1)
+        for c in range(WO_CHUNKS):
+            wo_wait(e2, x, c)
+            go("inner", lambda c=c: wo_z(e2, x, c, 0, e))
         for c in range(WO_CHUNKS):
             wo_wait(z, other, c)
+            go("inner", lambda c=c: wo_z(z, other, c, 0, e))
             go("inner", lambda c=c: wo_z(z, other, c, 1, m))
-            go("inner", lambda c=c: wo_z(z, other, c, 0, e))
 
     @pl.when(is_end)
     def _():
-        for xx in (x, other):
-            for c in range(WO_CHUNKS):
-                wo_wait(n, xx, c)
-                if c < END_CHUNKS:
-                    go("end", lambda xx=xx, c=c: wo_cross(n, xx, c))
+        cross(e2, x)
 
     mix_wait(f, other)
     for hop in (1, 2):
@@ -674,10 +739,9 @@
 
     @pl.when(is_inner)
     def _():
-        for xx in (x, other):
-            for c in range(WO_CHUNKS):
-                wo_wait(e, xx, c)
-                go("inner", lambda xx=xx, c=c: wo_z(e, xx, c, 1, m))
+        for c in range(WO_CHUNKS):
+            wo_wait(e2, other, c)
+            go("inner", lambda c=c: wo_z(e2, other, c, 0, e))
 
     mix_wait(ahead, other)
     go("all", lambda: mix_send(ahead, other, 2))
@@ -686,15 +750,9 @@
         where = pl.ds(pl.multiple_of(h * half_cols + c * chunk, chunk), chunk)
         return pltpu.make_async_copy(out_buf.at[h, :, cols(c)], out.at[:, where], s_res.at[h, c])
 
-    @pl.when(is_inner)
-    def _():
-        for c in range(WO_CHUNKS):
-            wo_wait(m, other, c)
-            go("inner", lambda c=c: wo_z(m, other, c, 0, e))
-        for xx in (x, other):
-            for c in range(WO_CHUNKS):
-                wo_wait(e2, xx, c)
-                go("inner", lambda xx=xx, c=c: wo_z(e2, xx, c, 0, e))
+    @pl.when(is_end)
+    def _():
+        cross(n, other)
 
     for ff in (beside, across):
         for xx in (x, other):
@@ -702,12 +760,7 @@
 
     @pl.when(is_end)
     def _():
-        for j in (m, e2):
-            for xx in (x, other):
-                for c in range(WO_CHUNKS):
-                    wo_wait(j, xx, c)
-                    if c < END_CHUNKS:
-                        go("end", lambda j=j, xx=xx, c=c: wo_cross(j, xx, c))
+        cross(e2, other)
 
     def product(h, c, row_tile):
         return jnp.dot(
@@ -719,9 +772,9 @@
             out_away.at[c], out_buf.at[x, :, cols(c)], s_out.at[c], r_out.at[c], dev(f, z, other)
         )
 
-    def away_stage(kind, c):
+    def away_stage(c):
         out_away[c] = product(x, c, other)
-        go(kind, lambda: away(c))
+        away(c).start()
 
     def own_stage(h, c):
         out_buf[h, :, cols(c)] = product(h, c, x)
@@ -732,62 +785,67 @@
         remote(ref, ref, s_out.at[c], r_out.at[c], here).wait_recv()
         result(other, c).start()
 
-    for c in range(END_CHUNKS, WO_CHUNKS):
-        away_stage("all", c)
+    def settle(kind):
+        for make in pending["all"] + pending[kind]:
+            make().wait_send()
+        q_far_copy().wait_send()
+        for b in range(2):
+            q_send(b).wait_send()
+        if kind == "inner":
+            for xx in range(nx):
+                for hf in range(2):
+                    e_far_copy(xx, hf).wait_send()
+                    for b in range(2):
+                        e_send(b, xx, hf).wait_send()
+
+        @pl.when(z < nz - 1)
+        def _():
+            for xx in range(nx):
+                seg_next(xx).wait_send()
+            kv_next().wait_send()
+
+        @pl.when(z > 0)
+        def _():
+            for pair in pairs[1:]:
+                kv_send(0, *pair).wait_send()
+
+    order = [*range(END_CHUNKS, WO_CHUNKS), *range(END_CHUNKS)]
 
     @pl.when(is_inner)
     def _():
-        for c in range(END_CHUNKS):
-            away_stage("inner", c)
-
-    for c in range(WO_CHUNKS):
-        own_stage(x, c)
+        for c in order:
+            wo_wait(m, other, c)
+            go("inner", lambda c=c: wo_z(m, other, c, 0, e))
+            away_stage(c)
+        for c in order:
+            own_stage(x, c)
+        for c in order:
+            away_wait(c)
+        settle("inner")
+        for c in order:
+            away(c).wait_send()
 
     @pl.when(is_end)
     def _():
+        for c in order:
+            wo_wait(m, other, c)
+            if c < END_CHUNKS:
+                go("end", lambda c=c: wo_cross(m, other, c))
+            if c >= END_CHUNKS:
+                away_stage(c)
+        for c in order:
+            own_stage(x, c)
         for c in range(END_CHUNKS):
             wox_wait(z, other, c)
             for j in (n, m, e2):
                 for xx in range(nx):
                     wox_wait(j, xx, c)
             own_stage(other, c)
-
-    for c in range(END_CHUNKS, WO_CHUNKS):
-        away_wait(c)
-
-    @pl.when(is_inner)
-    def _():
-        for c in range(END_CHUNKS):
+        for c in range(END_CHUNKS, WO_CHUNKS):
             away_wait(c)
-
-    for make in pending["all"]:
-        make().wait_send()
-    for kind, cond in (("end", is_end), ("inner", is_inner)):
-        @pl.when(cond)
-        def _():
-            for make in pending[kind]:
-                make().wait_send()
-
-    for d in range(1, nf):
-        q_send(lax.rem(f + d, nf)).wait_send()
-
-    @pl.when(is_inner)
-    def _():
-        for d in range(1, nf):
-            for xx in range(nx):
-                for hf in range(2):
-                    e_send(lax.rem(f + d, nf), xx, hf).wait_send()
-
-    @pl.when(z < nz - 1)
-    def _():
-        for xx in range(nx):
-            seg_next(xx).wait_send()
-        kv_next().wait_send()
-
-    @pl.when(z > 0)
-    def _():
-        for pair in pairs[1:]:
-            kv_send(0, *pair).wait_send()
+        settle("end")
+        for c in range(END_CHUNKS, WO_CHUNKS):
+            away(c).wait_send()
 
     for h in range(nx):
         for c in range(WO_CHUNKS):
@@ -808,12 +866,14 @@
     anywhere = pl.BlockSpec(memory_space=pl.ANY)
     scratch = [
         pltpu.VMEM((rows, kdim), bf16),
-        pltpu.VMEM((nz, kdim, HD), bf16),
+        pltpu.VMEM((nz // 2, kdim, 2 * HD), bf16),
         pltpu.VMEM((nz * kvw, kdim), bf16),
         pltpu.VMEM((nx, heads * HD, part), bf16),
         pltpu.VMEM((2, nx, 1, tok), jnp.int32),
         pltpu.VMEM((nz, rows, HD), f32),
-        pltpu.VMEM((nf, rows, HD), f32),
+        pltpu.VMEM((nf // 2, rows, HD), f32),
+        pltpu.VMEM((rows, HD), f32),
+        pltpu.VMEM((rows, HD), f32),
         pltpu.VMEM((rows, nz * kvw), f32),
         pltpu.VMEM((nf, sub, nz * kvw), f32),
         pltpu.VMEM((sub, HD), bf16),
@@ -826,18 +886,21 @@
         pltpu.VMEM((WO_CHUNKS, tok, part // WO_CHUNKS), bf16),
         pltpu.VMEM((nx, 2, tok // 2, kdim * MOVED // 8), bf16),
         pltpu.VMEM((nz, nx, 2, tok // 2, HD), f32),
-        pltpu.VMEM((nf, nx, 2, tok // 2, HD), f32),
+        pltpu.VMEM((nf // 2, nx, 2, tok // 2, HD), f32),
+        pltpu.VMEM((nx, 2, tok // 2, HD), f32),
+        pltpu.VMEM((nx, 2, tok // 2, HD), f32),
         pltpu.VMEM((nx, 2, tok // 2, HD), f32),
         pltpu.VMEM((nx, 2, tok // 2, HD), f32),
         dma((7,)), dma, dma, dma((1 + nx,)), dma((2, nx)),
         dma((2, nz)), dma((nz,)), dma((2, nz)), dma((nz,)),
-        dma((nz,)), dma((nf,)), dma((nf,)), dma((nf,)),
+        dma((nf // 2,)), dma((nf // 2,)), dma, dma, dma((nf,)), dma((nf,)),
         dma((2, nx, nf)), dma((2, nx, nf)),
         dma((2, nz, nx, WO_CHUNKS)), dma((nz, nx, WO_CHUNKS)),
         dma((nz + 1, nx, WO_CHUNKS)), dma((nz, nx, WO_CHUNKS)),
         dma((3, nx, nf)), dma((nx, nf)),
         dma((WO_CHUNKS,)), dma((WO_CHUNKS,)), dma((nx, WO_CHUNKS)),
-        dma((2,)), dma((nx, 2)), dma((2,)), dma((nz, nx, 2)), dma((nf, nx, 2)),
+        dma((2,)), dma((nx, 2)), dma((2,)), dma((nf // 2, nx, 2)), dma((nf // 2, nx, 2)),
+        dma((nx, 2)), dma((nx, 2)),
         dma((nx, 2)), dma((nx, 2)),
     ]
     return pl.pallas_call(

time: 113 us -> 90.8 us (0.80)
  the two profiles are of different devices: /device:TPU:0 before, /device:TPU:1 now
where the time goes in v3:
time: 90.8 us; the launch traced here: 90.7 us
  Pallas kernels  88.4 us (97%)
  local copies, waits for them, and re-layouts  2.3 us (3%)
    pallas_call x1, Pallas kernels, fused_on_device(): pl.pallas_call(functools.partial(fused_kernel, nf, nz, nx), out_shape=jax...  88.4 us
    unnamed x1, local copies, waits for them, and re-layouts  2.3 us

profile of v3, /device:TPU:1, one launch (start us, length us, event | category | flops | bytes accessed | tf_op | source)
XLA Modules:
  0.0 90.7 jit_solution(4360560504879992852)
XLA Ops:
  0.0 88.4 %fused_sublayer.1 = bf16[256,2048]{1,0:T(8,128)(2,1)} custom-call(bf16[256,2048]{1,0:T(8,128)(2,1)} %hid.1, bf16[2048,128]{1,0:T(8,128)(2,1)} %wq.1, bf16[32,2048]{1,0:T(8,128)(2,1)} %bitcast.2, bf16[128,2048]{1,0:T(8,128)(2,1)} %wo.1, s32[1,256]{1,0:T(1,128)} %bitcast.3), custom_call_target="tpu_custom_call" | custom-call | tf_op jit(solution)/shard_map/fused_sublayer/pallas_call | solution.py:906
  88.4 2.3 %copy.7 = bf16[256,2048]{1,0:T(8,128)(2,1)} copy(bf16[256,2048]{1,0:T(8,128)(2,1)} %fused_sublayer.1) | data formatting | bytes 2097152

commit v4 on v3

--- a/solution.py
+++ b/solution.py
@@ -132,7 +132,7 @@
 NEG_POS = -1
 WO_CHUNKS = 4
 MOVED = 4
-END_CHUNKS = 2
+END_CHUNKS = 3
 
 
 def fused_kernel(
@@ -141,7 +141,7 @@
     q_part, q_mate, q_sum, q_far, kv_part, kv_recv, kv_piece, kv_all, mix_own, mix_buf, q_cos, q_sin,
     out_buf, out_away, h_end, e_part, e_mate, e_sum, e_far, e_back, q_in,
     s_loc, s_hid, r_hid, s_seg, r_seg, s_wkv, r_wkv, s_wq, r_wq,
-    s_q, r_q, s_qf, r_qf, s_kvp, r_kvp, s_kv, r_kv, s_wo, r_wo, s_wox, r_wox, s_mix, r_mix,
+    s_q, r_q, s_qf, r_qf, s_kvp, r_kvp, s_kv, r_kv, s_kn, s_wo, r_wo, s_wox, r_wox, s_mix, r_mix,
     s_out, r_out, s_res, s_he, r_he, s_hx, s_ep, r_ep, s_ef, r_ef, s_eb, r_eb,
 ):
     f = lax.axis_index("fsdp")
@@ -188,12 +188,6 @@
         return pl.ds(pl.multiple_of(ref * count, count), count)
 
     here = (f, s)
-    pending = {"all": [], "end": [], "inner": []}
-
-    def go(kind, make):
-        make().start()
-        pending[kind].append(make)
-
     def cols(c):
         return slice(c * chunk, (c + 1) * chunk)
 
@@ -225,7 +219,7 @@
 
     def wkv_z(j, d, target):
         ref = wkv_buf.at[tile(j, kvw)]
-        return remote(ref, ref, s_wkv.at[d, j], r_wkv.at[j], dev(f, target, x))
+        return remote(ref, ref, s_wkv.at[d], r_wkv.at[j], dev(f, target, x))
 
     def wkv_wait(j):
         wkv_z(j, 0, z).wait_recv()
@@ -235,7 +229,7 @@
 
     def wq_z(j, d, target):
         ref = wq_of(j, 0) if d else wq_of(j, moved)
-        return remote(ref, ref, s_wq.at[d, j], r_wq.at[j], dev(f, target, x))
+        return remote(ref, ref, s_wq.at[d], r_wq.at[j], dev(f, target, x))
 
     def wq_wait(j, d=1):
         wq_z(j, d, z).wait_recv()
@@ -243,46 +237,46 @@
     def he_z(hf):
         rows_of = pl.ds(pl.multiple_of(x * tok + hf * block, block), block)
         return remote(
-            h_buf.at[rows_of, 0:moved], h_end.at[x, hf], s_he.at[hf], r_he.at[x, hf], dev(f, n, x)
+            h_buf.at[rows_of, 0:moved], h_end.at[x, hf], s_he, r_he.at[x, hf], dev(f, n, x)
         )
 
     def he_x(hf):
         ref = h_end.at[x, hf]
-        return remote(ref, ref, s_hx.at[hf], r_he.at[x, hf], dev(f, z, other))
+        return remote(ref, ref, s_hx, r_he.at[x, hf], dev(f, z, other))
 
     def he_wait(xx, hf):
         ref = h_end.at[xx, hf]
-        remote(ref, ref, s_hx.at[hf], r_he.at[xx, hf], here).wait_recv()
+        remote(ref, ref, s_hx, r_he.at[xx, hf], here).wait_recv()
 
     def wo_unit(h, j, xx, c):
         return wo_buf.at[h, tile(j * nx + xx, HD), cols(c)]
 
     def wo_z(j, xx, c, d, target):
         ref = wo_unit(x, j, xx, c)
-        return remote(ref, ref, s_wo.at[d, j, xx, c], r_wo.at[j, xx, c], dev(f, target, x))
+        return remote(ref, ref, s_wo.at[d], r_wo.at[j, xx, c], dev(f, target, x))
 
     def wo_pair(c):
         ref = wo_unit(other, z, x, c)
-        return remote(ref, ref, s_wox.at[nz, x, c], r_wo.at[z, x, c], dev(f, z, other))
+        return remote(ref, ref, s_wox, r_wo.at[z, x, c], dev(f, z, other))
 
     def wo_wait(j, xx, c):
         ref = wo_unit(x, j, xx, c)
-        remote(ref, ref, s_wox.at[0, 0, c], r_wo.at[j, xx, c], here).wait_recv()
+        remote(ref, ref, s_wox, r_wo.at[j, xx, c], here).wait_recv()
 
     def wo_cross(j, xx, c):
         ref = wo_unit(x, j, xx, c)
-        return remote(ref, ref, s_wox.at[j, xx, c], r_wox.at[j, xx, c], dev(f, z, other))
-
-    def wox_wait(j, xx, c):
-        ref = wo_unit(other, j, xx, c)
-        remote(ref, ref, s_wox.at[0, 0, c], r_wox.at[j, xx, c], here).wait_recv()
+        return remote(ref, ref, s_wox, r_wox.at[c], dev(f, z, other))
+
+    def wox_wait(c):
+        ref = wo_buf.at[other, HD:, cols(c)]
+        remote(ref, ref, s_wox, r_wox.at[c], here).wait_recv()
 
     def seg_same():
-        return remote(seg_buf.at[1, x], seg_buf.at[1, x], s_seg.at[0], r_seg.at[1, x], dev(f, z, other))
+        return remote(seg_buf.at[1, x], seg_buf.at[1, x], s_seg.at[0], r_seg.at[1], dev(f, z, other))
 
     def seg_next(xx):
         return remote(
-            seg_buf.at[1, x], seg_buf.at[0, x], s_seg.at[1 + xx], r_seg.at[0, x], dev(f, z + 1, xx)
+            seg_buf.at[1, x], seg_buf.at[0, x], s_seg.at[1], r_seg.at[0], dev(f, z + 1, xx)
         )
 
     barrier = pltpu.get_barrier_semaphore()
@@ -308,19 +302,19 @@
 
     @pl.when(is_end)
     def _():
-        go("end", lambda: wkv_z(z, 1, n))
-        go("end", lambda: wq_z(z, 1, n))
+        wkv_z(z, 1, n).start()
+        wq_z(z, 1, n).start()
 
     @pl.when(is_inner)
     def _():
         for d, target in ((0, e), (1, m)):
-            go("inner", lambda d=d, target=target: wkv_z(z, d, target))
-            go("inner", lambda d=d, target=target: wq_z(z, d, target))
+            wkv_z(z, d, target).start()
+            wq_z(z, d, target).start()
 
     own_h.wait()
-    go("all", hid_send)
+    hid_send().start()
     own_seg.wait()
-    go("all", seg_same)
+    seg_same().start()
 
     @pl.when(z < nz - 1)
     def _():
@@ -333,18 +327,18 @@
     @pl.when(is_end)
     def _():
         for hf in range(2):
-            go("end", lambda hf=hf: he_z(hf))
-        for c in range(WO_CHUNKS):
-            go("end", lambda c=c: wo_z(z, x, c, 1, n))
-        for c in range(WO_CHUNKS):
-            go("end", lambda c=c: wo_pair(c))
+            he_z(hf).start()
+        for c in range(WO_CHUNKS):
+            wo_z(z, x, c, 1, n).start()
+        for c in range(WO_CHUNKS):
+            wo_pair(c).start()
         for c in range(END_CHUNKS):
-            go("end", lambda c=c: wo_cross(z, x, c))
+            wo_cross(z, x, c).start()
 
     @pl.when(is_inner)
     def _():
         for c in range(WO_CHUNKS):
-            go("inner", lambda c=c: wo_z(z, x, c, 0, e))
+            wo_z(z, x, c, 0, e).start()
 
     @pl.when(z == 0)
     def _():
@@ -377,13 +371,8 @@
 
     def q_send(j):
         return remote(
-            q_part.at[j], q_mate.at[lax.rem(j, 2)], s_q.at[lax.rem(j, 2)], r_q.at[lax.rem(j, 2)], dev(beside, z, x)
-        )
-
-    def q_mate_wait(j):
-        remote(
-            q_mate.at[lax.rem(j, 2)], q_mate.at[lax.rem(j, 2)], s_q.at[0], r_q.at[lax.rem(j, 2)], here
-        ).wait_recv()
+            q_part.at[j], q_mate.at[lax.rem(j, 2)], s_q, r_q, dev(beside, z, x)
+        )
 
     def q_far_copy():
         return remote(q_sum, q_far, s_qf, r_qf, dev(ahead, z, x))
@@ -403,23 +392,19 @@
     def q_relay(far):
         @pl.when(jnp.logical_not(near) if far else near)
         def _():
-            q_mate_wait(theirs)
+            remote(q_mate, q_mate, s_q, r_q, here).wait_recv()
             q_sum[...] = q_part[theirs] + q_mate[lax.rem(theirs, 2)]
             q_far_copy().start()
 
     def e_send(j, xx, hf):
         return remote(
             e_part.at[j, xx, hf], e_mate.at[lax.rem(j, 2), xx, hf],
-            s_ep.at[lax.rem(j, 2), xx, hf], r_ep.at[lax.rem(j, 2), xx, hf], dev(beside, z, x)
-        )
-
-    def e_mate_wait(j, xx, hf):
-        ref = e_mate.at[lax.rem(j, 2), xx, hf]
-        remote(ref, ref, s_ep.at[0, xx, hf], r_ep.at[lax.rem(j, 2), xx, hf], here).wait_recv()
+            s_ep, r_ep.at[xx, hf], dev(beside, z, x)
+        )
 
     def e_far_copy(xx, hf):
         return remote(
-            e_sum.at[xx, hf], e_far.at[xx, hf], s_ef.at[xx, hf], r_ef.at[xx, hf], dev(ahead, z, x)
+            e_sum.at[xx, hf], e_far.at[xx, hf], s_ef, r_ef.at[xx, hf], dev(ahead, z, x)
         )
 
     def e_project(xx, hf, j):
@@ -435,40 +420,40 @@
                 e_send(j // 2 * 2 + b, xx, hf).start()
 
     def e_relay(xx, hf):
-        e_mate_wait(theirs, xx, hf)
+        ref = e_mate.at[:, xx, hf]
+        remote(ref, ref, s_ep, r_ep.at[xx, hf], here).wait_recv()
         e_sum[xx, hf] = e_part[theirs, xx, hf] + e_mate[lax.rem(theirs, 2), xx, hf]
         e_far_copy(xx, hf).start()
 
     def e_return(xx, hf):
         return remote(
-            e_back.at[xx, hf], q_in.at[xx, hf], s_eb.at[xx, hf], r_eb.at[xx, hf], dev(f, e, x)
+            e_back.at[xx, hf], q_in.at[xx, hf], s_eb, r_eb, dev(f, e, x)
         )
 
     def e_collect(xx, hf):
-        e_mate_wait(mine, xx, hf)
         ref = e_far.at[xx, hf]
-        remote(ref, ref, s_ef.at[xx, hf], r_ef.at[xx, hf], here).wait_recv()
+        remote(ref, ref, s_ef, r_ef.at[xx, hf], here).wait_recv()
         e_back[xx, hf] = (
             e_part[mine, xx, hf] + e_mate[lax.rem(mine, 2), xx, hf] + e_far[xx, hf]
         )
-        go("inner", lambda: e_return(xx, hf))
+        e_return(xx, hf).start()
 
     @pl.when(is_inner)
     def _():
         wkv_wait(e)
-        go("inner", lambda: wkv_z(e, 1, m))
+        wkv_z(e, 1, m).start()
         wkv_wait(m)
-        go("inner", lambda: wkv_z(m, 0, e))
+        wkv_z(m, 0, e).start()
         wq_wait(e)
-        go("inner", lambda: wq_z(e, 1, m))
-        for c in range(WO_CHUNKS):
-            go("inner", lambda c=c: wo_z(z, x, c, 1, m))
+        wq_z(e, 1, m).start()
+        for c in range(WO_CHUNKS):
+            wo_z(z, x, c, 1, m).start()
         wq_wait(m)
-        go("inner", lambda: wq_z(m, 0, e))
+        wq_z(m, 0, e).start()
         wkv_wait(e2)
-        go("inner", lambda: wkv_z(e2, 0, e))
+        wkv_z(e2, 0, e).start()
         he_wait(x, 0)
-        go("inner", lambda: he_x(0))
+        he_x(0).start()
 
     hid_wait()
 
@@ -484,23 +469,17 @@
     def kvp_send(d):
         ff = lax.rem(f + d, nf)
         return remote(
-            kv_part.at[tile(ff, sub)], kv_recv.at[f], s_kvp.at[d - 1], r_kvp.at[f], (ff, s)
-        )
-
-    def kvp_wait(d):
-        ff = lax.rem(f + d, nf)
-        remote(
-            kv_part.at[tile(ff, sub)], kv_recv.at[ff], s_kvp.at[d - 1], r_kvp.at[ff], here
-        ).wait_recv()
+            kv_part.at[tile(ff, sub)], kv_recv.at[f], s_kvp, r_kvp, (ff, s)
+        )
 
     for d in range(1, nf):
-        go("all", lambda d=d: kvp_send(d))
+        kvp_send(d).start()
 
     @pl.when(is_inner)
     def _():
         q_project(z, 0)
         he_wait(x, 1)
-        go("inner", lambda: he_x(1))
+        he_x(1).start()
         q_relay(False)
         e_project(x, 0, z)
 
@@ -516,41 +495,56 @@
         q_relay(False)
 
     total = kv_part[tile(f, sub), :]
+    arrived = kv_recv.at[1:nf]
+    remote(arrived, arrived, s_kvp, r_kvp, here).wait_recv()
     for d in range(1, nf):
-        kvp_wait(d)
         total = total + kv_recv[lax.rem(f + d, nf)]
     partner = jnp.where(
         lane < quarter, pltpu.roll(total, HD - quarter, 1), pltpu.roll(total, quarter, 1)
     )
     kv_piece[...] = (total * kv_cos + partner * kv_sin).astype(bf16)
     piece_rows = tile(f, sub)
-    own_piece = pltpu.make_async_copy(kv_piece, kv_all.at[1, x, piece_rows], s_loc.at[6])
-    own_piece.start()
-
-    def kv_send(plane, dx, d):
-        ff, xx = lax.rem(f + d, nf), lax.rem(x + dx, nx)
-        slot = kv_all.at[plane, x, piece_rows]
-        return remote(
-            kv_piece if plane else slot, slot,
-            s_kv.at[plane, dx, d], r_kv.at[plane, x, f], dev(ff, z, xx),
-        )
+    kv_all[1, x, piece_rows] = kv_piece[...]
+
+    def kv_of(plane, ff, xx):
+        return kv_all.at[plane, xx, tile(ff, sub)]
+
+    def kv_hop(plane, ff, xx, hop):
+        target = (dev(f, z, other), dev(ahead, z, x), dev(beside, z, x))[hop]
+        ref = kv_of(plane, ff, xx)
+        slot = hop + (hop == 2 or xx is other)
+        return remote(ref, ref, s_kv.at[plane], r_kv.at[plane, slot], target)
+
+    def kv_first(plane):
+        for hop in range(3):
+            kv_hop(plane, f, x, hop).start()
+
+    def kv_second(plane):
+        kv_wait(plane, f, other, 0)
+        for hop in (1, 2):
+            kv_hop(plane, f, other, hop).start()
+        kv_wait(plane, ahead, x, 1)
+        kv_hop(plane, ahead, x, 2).start()
+
+    def kv_third(plane):
+        kv_wait(plane, ahead, other, 2)
+        kv_hop(plane, ahead, other, 2).start()
+
+    def kv_last(plane):
+        ref = kv_all.at[plane, x]
+        remote(ref, ref, s_kn, r_kv.at[plane, 3], here).wait_recv()
 
     def kv_next():
         return remote(
             kv_piece, kv_all.at[0, x, piece_rows],
-            s_kv.at[0, 0, 0], r_kv.at[0, x, f], dev(f, z + 1, x),
-        )
-
-    def kv_wait(plane, dx, d):
-        ff, xx = lax.rem(f + d, nf), lax.rem(x + dx, nx)
-        remote(
-            kv_piece, kv_all.at[plane, xx, tile(ff, sub)],
-            s_kv.at[plane, dx, d], r_kv.at[plane, xx, ff], here,
-        ).wait_recv()
-
-    pairs = [(dx, d) for dx in range(nx) for d in range(nf)]
-    for pair in pairs[1:]:
-        go("all", lambda pair=pair: kv_send(1, *pair))
+            s_kn, r_kv.at[0, 4], dev(f, z + 1, x),
+        )
+
+    def kv_wait(plane, ff, xx, slot):
+        ref = kv_of(plane, ff, xx)
+        remote(ref, ref, s_kn, r_kv.at[plane, slot], here).wait_recv()
+
+    kv_first(1)
 
     @pl.when(z < nz - 1)
     def _():
@@ -560,12 +554,12 @@
     def _():
         for c in range(WO_CHUNKS):
             wo_wait(z, other, c)
-            go("end", lambda c=c: wo_z(z, other, c, 1, n))
+            wo_z(z, other, c, 1, n).start()
 
     @pl.when(is_inner)
     def _():
         wq_wait(e2)
-        go("inner", lambda: wq_z(e2, 0, e))
+        wq_z(e2, 0, e).start()
         q_project(e2, 0)
         e_project(x, 0, e2)
         e_project(x, 1, z)
@@ -576,7 +570,6 @@
             e_relay(x, 0)
 
         e_relay(x, 1)
-        q_relay(True)
         he_wait(other, 0)
         e_project(other, 0, z)
         e_project(other, 0, e2)
@@ -584,53 +577,72 @@
 
     @pl.when(z > 0)
     def _():
-        kv_wait(0, 0, 0)
-        for pair in pairs[1:]:
-            kv_send(0, *pair).start()
+        kv_wait(0, f, x, 4)
+        kv_first(0)
+
+    kv_second(1)
 
     @pl.when(is_inner)
     def _():
         for c in range(WO_CHUNKS):
-            go("inner", lambda c=c: wo_pair(c))
+            wo_pair(c).start()
         for c in range(WO_CHUNKS):
             wo_wait(e, x, c)
-            go("inner", lambda c=c: wo_z(e, x, c, 1, m))
+            wo_z(e, x, c, 1, m).start()
         e_collect(x, 0)
         he_wait(other, 1)
         e_project(other, 1, z)
         e_project(other, 1, e2)
+        e_relay(other, 1)
+        q_relay(True)
         for c in range(WO_CHUNKS):
             wo_wait(m, x, c)
-            go("inner", lambda c=c: wo_z(m, x, c, 0, e))
+            wo_z(m, x, c, 0, e).start()
+        kv_third(1)
+
+        @pl.when(z > 0)
+        def _():
+            kv_second(0)
+
         e_collect(other, 0)
-        e_relay(other, 1)
         e_collect(x, 1)
         for c in range(WO_CHUNKS):
             wo_wait(e, other, c)
-            go("inner", lambda c=c: wo_z(e, other, c, 1, m))
+            wo_z(e, other, c, 1, m).start()
+
+        @pl.when(z > 0)
+        def _():
+            kv_third(0)
+
         e_collect(other, 1)
 
     def cross(j, xx):
         for c in range(WO_CHUNKS):
             wo_wait(j, xx, c)
             if c < END_CHUNKS:
-                go("end", lambda c=c: wo_cross(j, xx, c))
+                wo_cross(j, xx, c).start()
 
     @pl.when(is_end)
     def _():
         cross(n, x)
+        kv_third(1)
+
+        @pl.when(z > 0)
+        def _():
+            kv_second(0)
+
         wq_wait(m, 0)
         wq_wait(e2, 0)
         q_project(e2, moved)
         q_relay(True)
+
+        @pl.when(z > 0)
+        def _():
+            kv_third(0)
+
         cross(m, x)
-        for xx in range(nx):
-            for hf in range(2):
-                remote(
-                    q_in.at[xx, hf], q_in.at[xx, hf], s_eb.at[xx, hf], r_eb.at[xx, hf], here
-                ).wait_recv()
-
-    q_mate_wait(mine)
+        remote(q_in, q_in, s_eb, r_eb, here).wait_recv()
+
     remote(q_far, q_far, s_qf, r_qf, here).wait_recv()
     q_total = q_part[mine] + q_mate[lax.rem(mine, 2)] + q_far[...]
     returned = q_in[...].reshape(rows, HD)
@@ -644,20 +656,15 @@
         picked = jnp.where(lane < quarter, first, jnp.where(lane < half, second, 0.0))
         quarters.append(picked.astype(bf16))
 
-    seg_wait = lambda plane, xx: remote(
-        seg_buf.at[plane, xx], seg_buf.at[plane, xx], s_seg.at[0], r_seg.at[plane, xx], here
-    ).wait_recv()
-    seg_wait(1, other)
-    own_piece.wait()
-    for pair in pairs[1:]:
-        kv_wait(1, *pair)
+    seg_ref = seg_buf.at[1, other]
+    remote(seg_ref, seg_ref, s_seg.at[0], r_seg.at[1], here).wait_recv()
+    kv_last(1)
 
     @pl.when(z > 0)
     def _():
-        for xx in range(nx):
-            seg_wait(0, xx)
-        for pair in pairs[1:]:
-            kv_wait(0, *pair)
+        before = seg_buf.at[0]
+        remote(before, before, s_seg.at[1], r_seg.at[0], here).wait_recv()
+        kv_last(0)
 
     key_seg = jnp.concatenate(
         [seg_buf[plane, xx] for plane in range(2) for xx in range(nx)], axis=1
@@ -705,58 +712,55 @@
     def mix_send(ff, xx, hop):
         target = (dev(f, z, other), dev(ahead, z, x), dev(beside, z, x))[hop]
         return remote(
-            mix_of(ff, xx), mix_of(ff, xx), s_mix.at[hop, xx, ff], r_mix.at[xx, ff], target
-        )
-
-    def mix_wait(ff, xx):
-        remote(
-            mix_of(ff, xx), mix_of(ff, xx), s_mix.at[0, xx, ff], r_mix.at[xx, ff], here
-        ).wait_recv()
+            mix_of(ff, xx), mix_of(ff, xx), s_mix,
+            r_mix.at[hop + (hop == 2 or xx is other)], target,
+        )
+
+    def mix_wait(ref, slot):
+        remote(ref, ref, s_mix, r_mix.at[slot], here).wait_recv()
 
     mix_buf[:, tile(head, HD)] = mix_own[...]
     for hop in range(3):
-        go("all", lambda hop=hop: mix_send(f, x, hop))
+        mix_send(f, x, hop).start()
 
     @pl.when(is_inner)
     def _():
         for c in range(WO_CHUNKS):
             wo_wait(e2, x, c)
-            go("inner", lambda c=c: wo_z(e2, x, c, 0, e))
+            wo_z(e2, x, c, 0, e).start()
         for c in range(WO_CHUNKS):
             wo_wait(z, other, c)
-            go("inner", lambda c=c: wo_z(z, other, c, 0, e))
-            go("inner", lambda c=c: wo_z(z, other, c, 1, m))
+            wo_z(z, other, c, 0, e).start()
+            wo_z(z, other, c, 1, m).start()
 
     @pl.when(is_end)
     def _():
         cross(e2, x)
 
-    mix_wait(f, other)
+    mix_wait(mix_of(f, other), 0)
     for hop in (1, 2):
-        go("all", lambda hop=hop: mix_send(f, other, hop))
-    mix_wait(ahead, x)
-    go("all", lambda: mix_send(ahead, x, 2))
+        mix_send(f, other, hop).start()
+    mix_wait(mix_of(ahead, x), 1)
+    mix_send(ahead, x, 2).start()
 
     @pl.when(is_inner)
     def _():
         for c in range(WO_CHUNKS):
             wo_wait(e2, other, c)
-            go("inner", lambda c=c: wo_z(e2, other, c, 0, e))
-
-    mix_wait(ahead, other)
-    go("all", lambda: mix_send(ahead, other, 2))
+            wo_z(e2, other, c, 0, e).start()
+
+    mix_wait(mix_of(ahead, other), 2)
+    mix_send(ahead, other, 2).start()
 
     def result(h, c):
         where = pl.ds(pl.multiple_of(h * half_cols + c * chunk, chunk), chunk)
-        return pltpu.make_async_copy(out_buf.at[h, :, cols(c)], out.at[:, where], s_res.at[h, c])
+        return pltpu.make_async_copy(out_buf.at[h, :, cols(c)], out.at[:, where], s_res)
 
     @pl.when(is_end)
     def _():
         cross(n, other)
 
-    for ff in (beside, across):
-        for xx in (x, other):
-            mix_wait(ff, xx)
+    mix_wait(mix_buf.at[:, 0 : 4 * HD], 3)
 
     @pl.when(is_end)
     def _():
@@ -769,7 +773,7 @@
 
     def away(c):
         return remote(
-            out_away.at[c], out_buf.at[x, :, cols(c)], s_out.at[c], r_out.at[c], dev(f, z, other)
+            out_away.at[c], out_buf.at[x, :, cols(c)], s_out, r_out.at[c], dev(f, z, other)
         )
 
     def away_stage(c):
@@ -782,32 +786,47 @@
 
     def away_wait(c):
         ref = out_buf.at[other, :, cols(c)]
-        remote(ref, ref, s_out.at[c], r_out.at[c], here).wait_recv()
+        remote(ref, ref, s_out, r_out.at[c], here).wait_recv()
         result(other, c).start()
 
+    def drained(sem, size):
+        ruler = wo_buf.at[0, 0 : size // (half_cols * 2), :]
+        remote(ruler, ruler, sem, r_hid, here).wait_send()
+
     def settle(kind):
-        for make in pending["all"] + pending[kind]:
-            make().wait_send()
-        q_far_copy().wait_send()
-        for b in range(2):
-            q_send(b).wait_send()
-        if kind == "inner":
-            for xx in range(nx):
-                for hf in range(2):
-                    e_far_copy(xx, hf).wait_send()
-                    for b in range(2):
-                        e_send(b, xx, hf).wait_send()
+        inner = kind == "inner"
+        unit = HD * chunk * 2
+        drained(s_hid, tok * kdim * 2)
+        drained(s_wkv.at[1], (2 if inner else 1) * kvw * kdim * 2)
+        drained(s_wq.at[1], (2 if inner else 1) * kdim * HD * 2)
+        drained(s_wo.at[1], (2 if inner else 1) * nx * WO_CHUNKS * unit)
+        crossed = 0 if inner else (nz * nx - 1) * END_CHUNKS
+        drained(s_wox, (WO_CHUNKS + crossed) * unit)
+        drained(s_hx if inner else s_he, 2 * block * moved * 2)
+        drained(s_q, 2 * rows * HD * 4)
+        drained(s_qf, rows * HD * 4)
+        drained(s_kvp, (nf - 1) * sub * nz * kvw * 4)
+        drained(s_kv.at[1], (nf * nx - 1) * sub * HD * 2)
+        drained(s_mix, (nf * nx - 1) * rows * HD * 2)
+        drained(s_out, (WO_CHUNKS if inner else WO_CHUNKS - END_CHUNKS) * tok * chunk * 2)
+        if inner:
+            drained(s_wkv.at[0], 3 * kvw * kdim * 2)
+            drained(s_wq.at[0], 3 * (kdim - moved) * HD * 2)
+            drained(s_wo.at[0], 3 * nx * WO_CHUNKS * unit)
+            drained(s_ep, 2 * rows * HD * 4)
+            drained(s_ef, rows * HD * 4)
+            drained(s_eb, rows * HD * 4)
+        seg_same().wait_send()
 
         @pl.when(z < nz - 1)
         def _():
-            for xx in range(nx):
-                seg_next(xx).wait_send()
+            before = seg_buf.at[0]
+            remote(before, before, s_seg.at[1], r_seg.at[0], here).wait_send()
             kv_next().wait_send()
 
         @pl.when(z > 0)
         def _():
-            for pair in pairs[1:]:
-                kv_send(0, *pair).wait_send()
+            drained(s_kv.at[0], (nf * nx - 1) * sub * HD * 2)
 
     order = [*range(END_CHUNKS, WO_CHUNKS), *range(END_CHUNKS)]
 
@@ -815,41 +834,33 @@
     def _():
         for c in order:
             wo_wait(m, other, c)
-            go("inner", lambda c=c: wo_z(m, other, c, 0, e))
+            wo_z(m, other, c, 0, e).start()
             away_stage(c)
         for c in order:
             own_stage(x, c)
         for c in order:
             away_wait(c)
         settle("inner")
-        for c in order:
-            away(c).wait_send()
 
     @pl.when(is_end)
     def _():
         for c in order:
             wo_wait(m, other, c)
             if c < END_CHUNKS:
-                go("end", lambda c=c: wo_cross(m, other, c))
+                wo_cross(m, other, c).start()
             if c >= END_CHUNKS:
                 away_stage(c)
         for c in order:
             own_stage(x, c)
         for c in range(END_CHUNKS):
-            wox_wait(z, other, c)
-            for j in (n, m, e2):
-                for xx in range(nx):
-                    wox_wait(j, xx, c)
+            wox_wait(c)
             own_stage(other, c)
         for c in range(END_CHUNKS, WO_CHUNKS):
             away_wait(c)
         settle("end")
-        for c in range(END_CHUNKS, WO_CHUNKS):
-            away(c).wait_send()
-
-    for h in range(nx):
-        for c in range(WO_CHUNKS):
-            result(h, c).wait()
+
+    ruler = wo_buf.at[0, 0 : tok * nx, :]
+    pltpu.make_async_copy(ruler, ruler, s_res).wait()
 
 
 def fused_on_device(nf, nz, nx, hidden, w_query, w_keyvalue, w_output, segment_ids):
@@ -891,17 +902,11 @@
         pltpu.VMEM((nx, 2, tok // 2, HD), f32),
         pltpu.VMEM((nx, 2, tok // 2, HD), f32),
         pltpu.VMEM((nx, 2, tok // 2, HD), f32),
-        dma((7,)), dma, dma, dma((1 + nx,)), dma((2, nx)),
-        dma((2, nz)), dma((nz,)), dma((2, nz)), dma((nz,)),
-        dma((nf // 2,)), dma((nf // 2,)), dma, dma, dma((nf,)), dma((nf,)),
-        dma((2, nx, nf)), dma((2, nx, nf)),
-        dma((2, nz, nx, WO_CHUNKS)), dma((nz, nx, WO_CHUNKS)),
-        dma((nz + 1, nx, WO_CHUNKS)), dma((nz, nx, WO_CHUNKS)),
-        dma((3, nx, nf)), dma((nx, nf)),
-        dma((WO_CHUNKS,)), dma((WO_CHUNKS,)), dma((nx, WO_CHUNKS)),
-        dma((2,)), dma((nx, 2)), dma((2,)), dma((nf // 2, nx, 2)), dma((nf // 2, nx, 2)),
-        dma((nx, 2)), dma((nx, 2)),
-        dma((nx, 2)), dma((nx, 2)),
+        dma((6,)), dma, dma, dma((2,)), dma((2,)), dma((2,)), dma((nz,)), dma((2,)), dma((nz,)),
+        dma, dma, dma, dma, dma, dma, dma((2,)), dma((2, 5)), dma,
+        dma((2,)), dma((nz, nx, WO_CHUNKS)), dma, dma((WO_CHUNKS,)), dma, dma((4,)),
+        dma, dma((WO_CHUNKS,)), dma, dma, dma((nx, 2)), dma,
+        dma, dma((nx, 2)), dma, dma((nx, 2)), dma, dma,
     ]
     return pl.pallas_call(
         functools.partial(fused_kernel, nf, nz, nx),

time: 90.8 us -> 87.8 us (0.967)
  the two profiles are of different devices: /device:TPU:1 before, /device:TPU:0 now
where the time goes in v4:
time: 87.8 us; the launch traced here: 87.7 us
  Pallas kernels  85.3 us (97%)
  local copies, waits for them, and re-layouts  2.3 us (3%)
    pallas_call x1, Pallas kernels, fused_on_device(): pl.pallas_call(functools.partial(fused_kernel, nf, nz, nx), out_shape=jax...  85.3 us
    unnamed x1, local copies, waits for them, and re-layouts  2.3 us

profile of v4, /device:TPU:0, one launch (start us, length us, event | category | flops | bytes accessed | tf_op | source)
XLA Modules:
  0.0 87.7 jit_solution(16577492799980850222)
XLA Ops:
  0.0 85.3 %fused_sublayer.1 = bf16[256,2048]{1,0:T(8,128)(2,1)} custom-call(bf16[256,2048]{1,0:T(8,128)(2,1)} %hid.1, bf16[2048,128]{1,0:T(8,128)(2,1)} %wq.1, bf16[32,2048]{1,0:T(8,128)(2,1)} %bitcast.2, bf16[128,2048]{1,0:T(8,128)(2,1)} %wo.1, s32[1,256]{1,0:T(1,128)} %bitcast.3), custom_call_target="tpu_custom_call" | custom-call | tf_op jit(solution)/shard_map/fused_sublayer/pallas_call | solution.py:911
  85.4 2.3 %copy.7 = bf16[256,2048]{1,0:T(8,128)(2,1)} copy(bf16[256,2048]{1,0:T(8,128)(2,1)} %fused_sublayer.1) | data formatting | bytes 2097152

commit v5 on v4

--- a/solution.py
+++ b/solution.py
@@ -141,7 +141,7 @@
     q_part, q_mate, q_sum, q_far, kv_part, kv_recv, kv_piece, kv_all, mix_own, mix_buf, q_cos, q_sin,
     out_buf, out_away, h_end, e_part, e_mate, e_sum, e_far, e_back, q_in,
     s_loc, s_hid, r_hid, s_seg, r_seg, s_wkv, r_wkv, s_wq, r_wq,
-    s_q, r_q, s_qf, r_qf, s_kvp, r_kvp, s_kv, r_kv, s_kn, s_wo, r_wo, s_wox, r_wox, s_mix, r_mix,
+    s_q, r_q, s_qf, r_qf, s_kvp, r_kvp, s_kv, r_kv, s_kn, s_wo, r_wo, r_rest, s_wox, r_wox, s_mix, r_mix,
     s_out, r_out, s_res, s_he, r_he, s_hx, s_ep, r_ep, s_ef, r_ef, s_eb, r_eb,
 ):
     f = lax.axis_index("fsdp")
@@ -224,15 +224,13 @@
     def wkv_wait(j):
         wkv_z(j, 0, z).wait_recv()
 
-    def wq_of(j, first):
-        return wq_buf.at[j // 2, first:, tile(lax.rem(j, 2), HD)]
-
-    def wq_z(j, d, target):
-        ref = wq_of(j, 0) if d else wq_of(j, moved)
-        return remote(ref, ref, s_wq.at[d], r_wq.at[j], dev(f, target, x))
-
-    def wq_wait(j, d=1):
-        wq_z(j, d, z).wait_recv()
+    def wq_z(j, part, d, target):
+        features = slice(moved, kdim) if part == 0 else slice(0, moved)
+        ref = wq_buf.at[j // 2, features, tile(lax.rem(j, 2), HD)]
+        return remote(ref, ref, s_wq.at[d], r_wq.at[j, part], dev(f, target, x))
+
+    def wq_wait(j, part):
+        wq_z(j, part, 1, z).wait_recv()
 
     def he_z(hf):
         rows_of = pl.ds(pl.multiple_of(x * tok + hf * block, block), block)
@@ -267,8 +265,17 @@
         ref = wo_unit(x, j, xx, c)
         return remote(ref, ref, s_wox, r_wox.at[c], dev(f, z, other))
 
+    def wo_rest(c):
+        ref = wo_unit(other, n, x, c)
+        return remote(ref, ref, s_wo.at[0], r_rest.at[c], dev(f, e, x))
+
+    def wo_swap(c):
+        ref = wo_unit(other, n, x, c)
+        remote(ref, ref, s_wox, r_rest.at[c], here).wait_recv()
+        return remote(ref, ref, s_wox, r_wo.at[n, x, c], dev(f, z, other))
+
     def wox_wait(c):
-        ref = wo_buf.at[other, HD:, cols(c)]
+        ref = wo_buf.at[other, 2 * HD :, cols(c)]
         remote(ref, ref, s_wox, r_wox.at[c], here).wait_recv()
 
     def seg_same():
@@ -303,13 +310,15 @@
     @pl.when(is_end)
     def _():
         wkv_z(z, 1, n).start()
-        wq_z(z, 1, n).start()
+        wq_z(z, 0, 1, n).start()
+        wq_z(z, 1, 1, n).start()
 
     @pl.when(is_inner)
     def _():
         for d, target in ((0, e), (1, m)):
             wkv_z(z, d, target).start()
-            wq_z(z, d, target).start()
+            wq_z(z, 0, d, target).start()
+        wq_z(z, 1, 1, m).start()
 
     own_h.wait()
     hid_send().start()
@@ -444,16 +453,20 @@
         wkv_z(e, 1, m).start()
         wkv_wait(m)
         wkv_z(m, 0, e).start()
-        wq_wait(e)
-        wq_z(e, 1, m).start()
-        for c in range(WO_CHUNKS):
-            wo_z(z, x, c, 1, m).start()
-        wq_wait(m)
-        wq_z(m, 0, e).start()
+        wq_wait(e, 0)
+        wq_z(e, 0, 1, m).start()
+        wq_wait(m, 0)
+        wq_z(m, 0, 0, e).start()
+        wq_wait(e, 1)
+        wq_z(e, 1, 1, m).start()
         wkv_wait(e2)
         wkv_z(e2, 0, e).start()
         he_wait(x, 0)
         he_x(0).start()
+        wq_wait(e2, 0)
+        wq_z(e2, 0, 0, e).start()
+        for c in range(WO_CHUNKS):
+            wo_rest(c).start()
 
     hid_wait()
 
@@ -558,8 +571,10 @@
 
     @pl.when(is_inner)
     def _():
-        wq_wait(e2)
-        wq_z(e2, 0, e).start()
+        for c in range(WO_CHUNKS):
+            wo_z(z, x, c, 1, m).start()
+        wq_wait(m, 1)
+        wq_wait(e2, 1)
         q_project(e2, 0)
         e_project(x, 0, e2)
         e_project(x, 1, z)
@@ -606,6 +621,7 @@
 
         e_collect(other, 0)
         e_collect(x, 1)
+        e_collect(other, 1)
         for c in range(WO_CHUNKS):
             wo_wait(e, other, c)
             wo_z(e, other, c, 1, m).start()
@@ -614,7 +630,9 @@
         def _():
             kv_third(0)
 
-        e_collect(other, 1)
+        for c in range(WO_CHUNKS):
+            wo_wait(e2, x, c)
+            wo_z(e2, x, c, 0, e).start()
 
     def cross(j, xx):
         for c in range(WO_CHUNKS):
@@ -640,6 +658,8 @@
         def _():
             kv_third(0)
 
+        for c in range(WO_CHUNKS):
+            wo_swap(c).start()
         cross(m, x)
         remote(q_in, q_in, s_eb, r_eb, here).wait_recv()
 
@@ -726,11 +746,7 @@
     @pl.when(is_inner)
     def _():
         for c in range(WO_CHUNKS):
-            wo_wait(e2, x, c)
-            wo_z(e2, x, c, 0, e).start()
-        for c in range(WO_CHUNKS):
             wo_wait(z, other, c)
-            wo_z(z, other, c, 0, e).start()
             wo_z(z, other, c, 1, m).start()
 
     @pl.when(is_end)
@@ -749,6 +765,12 @@
             wo_wait(e2, other, c)
             wo_z(e2, other, c, 0, e).start()
 
+    @pl.when(is_end)
+    def _():
+        for c in range(WO_CHUNKS):
+            wo_wait(n, other, c)
+        cross(e2, other)
+
     mix_wait(mix_of(ahead, other), 2)
     mix_send(ahead, other, 2).start()
 
@@ -756,15 +778,7 @@
         where = pl.ds(pl.multiple_of(h * half_cols + c * chunk, chunk), chunk)
         return pltpu.make_async_copy(out_buf.at[h, :, cols(c)], out.at[:, where], s_res)
 
-    @pl.when(is_end)
-    def _():
-        cross(n, other)
-
     mix_wait(mix_buf.at[:, 0 : 4 * HD], 3)
-
-    @pl.when(is_end)
-    def _():
-        cross(e2, other)
 
     def product(h, c, row_tile):
         return jnp.dot(
@@ -800,7 +814,7 @@
         drained(s_wkv.at[1], (2 if inner else 1) * kvw * kdim * 2)
         drained(s_wq.at[1], (2 if inner else 1) * kdim * HD * 2)
         drained(s_wo.at[1], (2 if inner else 1) * nx * WO_CHUNKS * unit)
-        crossed = 0 if inner else (nz * nx - 1) * END_CHUNKS
+        crossed = 0 if inner else (nz * nx - 2) * END_CHUNKS + WO_CHUNKS
         drained(s_wox, (WO_CHUNKS + crossed) * unit)
         drained(s_hx if inner else s_he, 2 * block * moved * 2)
         drained(s_q, 2 * rows * HD * 4)
@@ -902,9 +916,10 @@
         pltpu.VMEM((nx, 2, tok // 2, HD), f32),
         pltpu.VMEM((nx, 2, tok // 2, HD), f32),
         pltpu.VMEM((nx, 2, tok // 2, HD), f32),
-        dma((6,)), dma, dma, dma((2,)), dma((2,)), dma((2,)), dma((nz,)), dma((2,)), dma((nz,)),
+        dma((6,)), dma, dma, dma((2,)), dma((2,)), dma((2,)), dma((nz,)), dma((2,)), dma((nz, 2)),
         dma, dma, dma, dma, dma, dma, dma((2,)), dma((2, 5)), dma,
-        dma((2,)), dma((nz, nx, WO_CHUNKS)), dma, dma((WO_CHUNKS,)), dma, dma((4,)),
+        dma((2,)), dma((nz, nx, WO_CHUNKS)), dma((WO_CHUNKS,)), dma, dma((WO_CHUNKS,)), dma,
+        dma((4,)),
         dma, dma((WO_CHUNKS,)), dma, dma, dma((nx, 2)), dma,
         dma, dma((nx, 2)), dma, dma((nx, 2)), dma, dma,
     ]

time: 87.8 us -> 82.8 us (0.943)
  Pallas kernels: 85.3 us -> 80.3 us
    pallas_call x1, Pallas kernels: 85.3 us -> 80.3 us  [fused_on_device(): pl.pallas_call(functools.partial(fused_kernel, nf, nz, nx), out_shape=jax...]
where the time goes in v5:
time: 82.8 us; the launch traced here: 82.7 us
  Pallas kernels  80.3 us (97%)
  local copies, waits for them, and re-layouts  2.3 us (3%)
    pallas_call x1, Pallas kernels, fused_on_device(): pl.pallas_call(functools.partial(fused_kernel, nf, nz, nx), out_shape=jax...  80.3 us
    unnamed x1, local copies, waits for them, and re-layouts  2.3 us

profile of v5, /device:TPU:0, one launch (start us, length us, event | category | flops | bytes accessed | tf_op | source)
XLA Modules:
  0.0 82.7 jit_solution(17817954213670616635)
XLA Ops:
  0.0 80.3 %fused_sublayer.1 = bf16[256,2048]{1,0:T(8,128)(2,1)} custom-call(bf16[256,2048]{1,0:T(8,128)(2,1)} %hid.1, bf16[2048,128]{1,0:T(8,128)(2,1)} %wq.1, bf16[32,2048]{1,0:T(8,128)(2,1)} %bitcast.2, bf16[128,2048]{1,0:T(8,128)(2,1)} %wo.1, s32[1,256]{1,0:T(1,128)} %bitcast.3), custom_call_target="tpu_custom_call" | custom-call | tf_op jit(solution)/shard_map/fused_sublayer/pallas_call | solution.py:926
  80.4 2.3 %copy.7 = bf16[256,2048]{1,0:T(8,128)(2,1)} copy(bf16[256,2048]{1,0:T(8,128)(2,1)} %fused_sublayer.1) | data formatting | bytes 2097152

commit v6 on v5

--- a/solution.py
+++ b/solution.py
@@ -133,12 +133,13 @@
 WO_CHUNKS = 4
 MOVED = 4
 END_CHUNKS = 3
+INNER_CHUNKS = 1
 
 
 def fused_kernel(
     nf, nz, nx, hid, wq, wkv, wo, seg, out,
     h_buf, wq_buf, wkv_buf, wo_buf, seg_buf,
-    q_part, q_mate, q_sum, q_far, kv_part, kv_recv, kv_piece, kv_all, mix_own, mix_buf, q_cos, q_sin,
+    q_part, q_mate, q_sum, q_far, kv_part, kv_recv, kv_piece, kv_all, mix_buf, q_cos, q_sin,
     out_buf, out_away, h_end, e_part, e_mate, e_sum, e_far, e_back, q_in,
     s_loc, s_hid, r_hid, s_seg, r_seg, s_wkv, r_wkv, s_wq, r_wq,
     s_q, r_q, s_qf, r_qf, s_kvp, r_kvp, s_kv, r_kv, s_kn, s_wo, r_wo, r_rest, s_wox, r_wox, s_mix, r_mix,
@@ -274,8 +275,8 @@
         remote(ref, ref, s_wox, r_rest.at[c], here).wait_recv()
         return remote(ref, ref, s_wox, r_wo.at[n, x, c], dev(f, z, other))
 
-    def wox_wait(c):
-        ref = wo_buf.at[other, 2 * HD :, cols(c)]
+    def wox_wait(c, held):
+        ref = wo_buf.at[other, held * HD :, cols(c)]
         remote(ref, ref, s_wox, r_wox.at[c], here).wait_recv()
 
     def seg_same():
@@ -601,9 +602,13 @@
     def _():
         for c in range(WO_CHUNKS):
             wo_pair(c).start()
+        for c in range(INNER_CHUNKS):
+            wo_cross(z, x, c).start()
         for c in range(WO_CHUNKS):
             wo_wait(e, x, c)
             wo_z(e, x, c, 1, m).start()
+            if c < INNER_CHUNKS:
+                wo_cross(e, x, c).start()
         e_collect(x, 0)
         he_wait(other, 1)
         e_project(other, 1, z)
@@ -613,6 +618,8 @@
         for c in range(WO_CHUNKS):
             wo_wait(m, x, c)
             wo_z(m, x, c, 0, e).start()
+            if c < INNER_CHUNKS:
+                wo_cross(m, x, c).start()
         kv_third(1)
 
         @pl.when(z > 0)
@@ -625,6 +632,8 @@
         for c in range(WO_CHUNKS):
             wo_wait(e, other, c)
             wo_z(e, other, c, 1, m).start()
+            if c < INNER_CHUNKS:
+                wo_cross(e, other, c).start()
 
         @pl.when(z > 0)
         def _():
@@ -633,6 +642,8 @@
         for c in range(WO_CHUNKS):
             wo_wait(e2, x, c)
             wo_z(e2, x, c, 0, e).start()
+            if c < INNER_CHUNKS:
+                wo_cross(e2, x, c).start()
 
     def cross(j, xx):
         for c in range(WO_CHUNKS):
@@ -695,6 +706,24 @@
     keys = [
         jnp.concatenate([kv_all[0, xx], kv_all[1, xx]], axis=0) for xx in range(nx)
     ]
+    head = mine * nx + x
+    half_rows = rows // 2
+
+    def mix_of(ff, xx, hf):
+        return mix_buf.at[
+            hf * half_rows : (hf + 1) * half_rows, tile(block_of(ff) * nx + xx, HD)
+        ]
+
+    def mix_send(ff, xx, hop, hf):
+        target = (dev(f, z, other), dev(ahead, z, x), dev(beside, z, x))[hop]
+        ref = mix_of(ff, xx, hf)
+        return remote(
+            ref, ref, s_mix, r_mix.at[hf, hop + (hop == 2 or xx is other)], target
+        )
+
+    def mix_wait(ref, slot, hf):
+        remote(ref, ref, s_mix, r_mix.at[hf, slot], here).wait_recv()
+
     step_rows = rows // nf
     for b in range(nf):
         span = slice(b * step_rows, (b + 1) * step_rows)
@@ -722,26 +751,10 @@
             lane_block = lane // quarter
             value = jnp.where(lane_block < nx, first, second)
             mixed = value if mixed is None else jnp.where(lane_block % nx == xx, value, mixed)
-        mix_own[span, :] = (mixed / row_total).astype(bf16)
-
-    head = mine * nx + x
-
-    def mix_of(ff, xx):
-        return mix_buf.at[:, tile(block_of(ff) * nx + xx, HD)]
-
-    def mix_send(ff, xx, hop):
-        target = (dev(f, z, other), dev(ahead, z, x), dev(beside, z, x))[hop]
-        return remote(
-            mix_of(ff, xx), mix_of(ff, xx), s_mix,
-            r_mix.at[hop + (hop == 2 or xx is other)], target,
-        )
-
-    def mix_wait(ref, slot):
-        remote(ref, ref, s_mix, r_mix.at[slot], here).wait_recv()
-
-    mix_buf[:, tile(head, HD)] = mix_own[...]
-    for hop in range(3):
-        mix_send(f, x, hop).start()
+        mix_buf[span, tile(head, HD)] = (mixed / row_total).astype(bf16)
+        if b % 2 == 1:
+            for hop in range(3):
+                mix_send(f, x, hop, b // 2).start()
 
     @pl.when(is_inner)
     def _():
@@ -749,21 +762,27 @@
             wo_wait(z, other, c)
             wo_z(z, other, c, 1, m).start()
 
+    def mix_relay(hf):
+        mix_wait(mix_of(f, other, hf), 0, hf)
+        for hop in (1, 2):
+            mix_send(f, other, hop, hf).start()
+        mix_wait(mix_of(ahead, x, hf), 1, hf)
+        mix_send(ahead, x, 2, hf).start()
+
     @pl.when(is_end)
     def _():
         cross(e2, x)
 
-    mix_wait(mix_of(f, other), 0)
-    for hop in (1, 2):
-        mix_send(f, other, hop).start()
-    mix_wait(mix_of(ahead, x), 1)
-    mix_send(ahead, x, 2).start()
+    mix_relay(0)
+    mix_relay(1)
 
     @pl.when(is_inner)
     def _():
         for c in range(WO_CHUNKS):
             wo_wait(e2, other, c)
             wo_z(e2, other, c, 0, e).start()
+            if c < INNER_CHUNKS:
+                wo_cross(e2, other, c).start()
 
     @pl.when(is_end)
     def _():
@@ -771,14 +790,16 @@
             wo_wait(n, other, c)
         cross(e2, other)
 
-    mix_wait(mix_of(ahead, other), 2)
-    mix_send(ahead, other, 2).start()
+    for hf in range(2):
+        mix_wait(mix_of(ahead, other, hf), 2, hf)
+        mix_send(ahead, other, 2, hf).start()
 
     def result(h, c):
         where = pl.ds(pl.multiple_of(h * half_cols + c * chunk, chunk), chunk)
         return pltpu.make_async_copy(out_buf.at[h, :, cols(c)], out.at[:, where], s_res)
 
-    mix_wait(mix_buf.at[:, 0 : 4 * HD], 3)
+    for hf in range(2):
+        mix_wait(mix_buf.at[0:half_rows, 0 : 4 * HD], 3, hf)
 
     def product(h, c, row_tile):
         return jnp.dot(
@@ -814,15 +835,12 @@
         drained(s_wkv.at[1], (2 if inner else 1) * kvw * kdim * 2)
         drained(s_wq.at[1], (2 if inner else 1) * kdim * HD * 2)
         drained(s_wo.at[1], (2 if inner else 1) * nx * WO_CHUNKS * unit)
-        crossed = 0 if inner else (nz * nx - 2) * END_CHUNKS + WO_CHUNKS
-        drained(s_wox, (WO_CHUNKS + crossed) * unit)
         drained(s_hx if inner else s_he, 2 * block * moved * 2)
         drained(s_q, 2 * rows * HD * 4)
         drained(s_qf, rows * HD * 4)
         drained(s_kvp, (nf - 1) * sub * nz * kvw * 4)
         drained(s_kv.at[1], (nf * nx - 1) * sub * HD * 2)
         drained(s_mix, (nf * nx - 1) * rows * HD * 2)
-        drained(s_out, (WO_CHUNKS if inner else WO_CHUNKS - END_CHUNKS) * tok * chunk * 2)
         if inner:
             drained(s_wkv.at[0], 3 * kvw * kdim * 2)
             drained(s_wq.at[0], 3 * (kdim - moved) * HD * 2)
@@ -842,6 +860,16 @@
         def _():
             drained(s_kv.at[0], (nf * nx - 1) * sub * HD * 2)
 
+    def settle_last(kind):
+        inner = kind == "inner"
+        unit = HD * chunk * 2
+        if inner:
+            crossed = (nz * nx - 1) * INNER_CHUNKS
+        else:
+            crossed = (nz * nx - 2) * END_CHUNKS + WO_CHUNKS
+        drained(s_wox, (WO_CHUNKS + crossed) * unit)
+        drained(s_out, (WO_CHUNKS - (INNER_CHUNKS if inner else END_CHUNKS)) * tok * chunk * 2)
+
     order = [*range(END_CHUNKS, WO_CHUNKS), *range(END_CHUNKS)]
 
     @pl.when(is_inner)
@@ -849,12 +877,19 @@
         for c in order:
             wo_wait(m, other, c)
             wo_z(m, other, c, 0, e).start()
-            away_stage(c)
+            if c < INNER_CHUNKS:
+                wo_cross(m, other, c).start()
+            else:
+                away_stage(c)
         for c in order:
             own_stage(x, c)
-        for c in order:
+        settle("inner")
+        for c in range(INNER_CHUNKS):
+            wox_wait(c, 1)
+            own_stage(other, c)
+        for c in range(INNER_CHUNKS, WO_CHUNKS):
             away_wait(c)
-        settle("inner")
+        settle_last("inner")
 
     @pl.when(is_end)
     def _():
@@ -866,12 +901,13 @@
                 away_stage(c)
         for c in order:
             own_stage(x, c)
+        settle("end")
         for c in range(END_CHUNKS):
-            wox_wait(c)
+            wox_wait(c, 2)
             own_stage(other, c)
         for c in range(END_CHUNKS, WO_CHUNKS):
             away_wait(c)
-        settle("end")
+        settle_last("end")
 
     ruler = wo_buf.at[0, 0 : tok * nx, :]
     pltpu.make_async_copy(ruler, ruler, s_res).wait()
@@ -903,7 +939,6 @@
         pltpu.VMEM((nf, sub, nz * kvw), f32),
         pltpu.VMEM((sub, HD), bf16),
         pltpu.VMEM((2, nx, rows, HD), bf16),
-        pltpu.VMEM((rows, HD), bf16),
         pltpu.VMEM((rows, heads * HD), bf16),
         pltpu.VMEM((rows, HD), f32),
         pltpu.VMEM((rows, HD), f32),
@@ -919,7 +954,7 @@
         dma((6,)), dma, dma, dma((2,)), dma((2,)), dma((2,)), dma((nz,)), dma((2,)), dma((nz, 2)),
         dma, dma, dma, dma, dma, dma, dma((2,)), dma((2, 5)), dma,
         dma((2,)), dma((nz, nx, WO_CHUNKS)), dma((WO_CHUNKS,)), dma, dma((WO_CHUNKS,)), dma,
-        dma((4,)),
+        dma((2, 4)),
         dma, dma((WO_CHUNKS,)), dma, dma, dma((nx, 2)), dma,
         dma, dma((nx, 2)), dma, dma((nx, 2)), dma, dma,
     ]

time: 82.8 us -> 82.7 us (level)
  no operation moved by 1% of the time
where the time goes in v6:
time: 82.7 us; the launch traced here: 82.5 us
  Pallas kernels  80.2 us (97%)
  local copies, waits for them, and re-layouts  2.3 us (3%)
    pallas_call x1, Pallas kernels, fused_on_device(): pl.pallas_call(functools.partial(fused_kernel, nf, nz, nx), out_shape=jax...  80.2 us
    unnamed x1, local copies, waits for them, and re-layouts  2.3 us

profile of v6, /device:TPU:0, one launch (start us, length us, event | category | flops | bytes accessed | tf_op | source)
XLA Modules:
  0.0 82.5 jit_solution(15021401388903707020)
XLA Ops:
  0.0 80.2 %fused_sublayer.1 = bf16[256,2048]{1,0:T(8,128)(2,1)} custom-call(bf16[256,2048]{1,0:T(8,128)(2,1)} %hid.1, bf16[2048,128]{1,0:T(8,128)(2,1)} %wq.1, bf16[32,2048]{1,0:T(8,128)(2,1)} %bitcast.2, bf16[128,2048]{1,0:T(8,128)(2,1)} %wo.1, s32[1,256]{1,0:T(1,128)} %bitcast.3), custom_call_target="tpu_custom_call" | custom-call | tf_op jit(solution)/shard_map/fused_sublayer/pallas_call | solution.py:961
  80.2 2.3 %copy.7 = bf16[256,2048]{1,0:T(8,128)(2,1)} copy(bf16[256,2048]{1,0:T(8,128)(2,1)} %fused_sublayer.1) | data formatting | bytes 2097152

commit v7 on v6

--- a/solution.py
+++ b/solution.py
@@ -870,7 +870,7 @@
         drained(s_wox, (WO_CHUNKS + crossed) * unit)
         drained(s_out, (WO_CHUNKS - (INNER_CHUNKS if inner else END_CHUNKS)) * tok * chunk * 2)
 
-    order = [*range(END_CHUNKS, WO_CHUNKS), *range(END_CHUNKS)]
+    order = [*range(WO_CHUNKS)]
 
     @pl.when(is_inner)
     def _():

time: 82.7 us -> 82.2 us (level)
  no operation moved by 1% of the time
where the time goes in v7:
time: 82.2 us; the launch traced here: 82 us
  Pallas kernels  79.7 us (97%)
  local copies, waits for them, and re-layouts  2.3 us (3%)
    pallas_call x1, Pallas kernels, fused_on_device(): pl.pallas_call(functools.partial(fused_kernel, nf, nz, nx), out_shape=jax...  79.7 us
    unnamed x1, local copies, waits for them, and re-layouts  2.3 us

profile of v7, /device:TPU:0, one launch (start us, length us, event | category | flops | bytes accessed | tf_op | source)
XLA Modules:
  0.0 82.0 jit_solution(274189792881309405)
XLA Ops:
  0.0 79.7 %fused_sublayer.1 = bf16[256,2048]{1,0:T(8,128)(2,1)} custom-call(bf16[256,2048]{1,0:T(8,128)(2,1)} %hid.1, bf16[2048,128]{1,0:T(8,128)(2,1)} %wq.1, bf16[32,2048]{1,0:T(8,128)(2,1)} %bitcast.2, bf16[128,2048]{1,0:T(8,128)(2,1)} %wo.1, s32[1,256]{1,0:T(1,128)} %bitcast.3), custom_call_target="tpu_custom_call" | custom-call | tf_op jit(solution)/shard_map/fused_sublayer/pallas_call | solution.py:961
  79.7 2.3 %copy.7 = bf16[256,2048]{1,0:T(8,128)(2,1)} copy(bf16[256,2048]{1,0:T(8,128)(2,1)} %fused_sublayer.1) | data formatting | bytes 2097152
